TPU v7x, 32 devices: a whole 2x2x4 slice. The times are simulated.
32 devices in a mesh: gx: 4 (over y, core), gy: 8 (over z, x).
Axes of the slice: x: 2, y: 2, z: 4, core: 2. Of those that a mesh axis runs over, the one named last changes fastest.
Arguments:
- child_value: bfloat16 [524288, 128], P(('gx', 'gy')), may hold values from -6 to 6
- child_row: int32 [32, 16384], P(('gx', 'gy')), may hold values from 0 to 16383, each once within a row
- opp_set: int32 [524288], P(('gx', 'gy')), may hold values from 0 to 65535, as said below
- opp_home: int32 [65536], replicated, may hold values from 0 to 65535, as said below
- opp_cum: float32 [65536, 128], P(('gx', 'gy')), may hold values from 0.01 to 1
- reach: float32 [4096], P(('gx', 'gy')), may hold values from 0.05 to 1
- br_set: int32 [4096], P(('gx', 'gy')), may hold values from 0 to 2047, as said below
- br_home: int32 [2048], replicated, may hold values from 0 to 2047, as said below
- br_cum: float32 [2048, 128], P(('gx', 'gy')), may hold values from 0.01 to 1
Outputs:
- history_value: float32 [524288], P(('gx', 'gy'))
- regret_gap: float32 [2048], P(('gx', 'gy'))
- exploitability: float32 [], replicated
Inputs may be any that keep to these rules, and one draw needn't show every extreme that they name: A permutation: opponent infoset i lives in row opp_home[i], owned by device opp_home[i] // 2048. `opp_set`: among the 16384 rows of one device at most 1024 have infosets owned by any one device; in every draw some owner has exactly 1024 from every device. A permutation: best-responder infoset i lives in row br_home[i], owned by device br_home[i] // 64. `br_set`: among the 128 rows of one device at most 8 have infosets owned by any one device; in every draw some owner has exactly 8 from every device.
All inputs are finite; a program needn't handle non-finite values.
Results may differ from a plain program's by a relative error of at most 0.0029.
Values may be sent and summed in bfloat16 or wider, within the bound.
No kernel may reach another device: no remote copies, remote signals or barrier semaphores. Data moves between devices by JAX's collectives and lax.ppermute only.
A program may use at most 128 MiB of HBM per device.

v0:
```python
import functools

import jax
import jax.numpy as jnp
from jax import lax
from jax.experimental import pallas as pl
from jax.experimental.pallas import tpu as pltpu
from jax.sharding import PartitionSpec as P


AXES = ("gx", "gy")
LANES = 128
SCALE_BITS = 17
TABLE_LIMIT = 24 * 2**20
SHARES = (5, 3, 6, 1, 1)


def iota(shape, dim):
    return lax.broadcasted_iota(jnp.int32, shape, dim)


def one_hot(hit):
    return jnp.where(hit, 1.0, 0.0).astype(jnp.bfloat16)


def room(size):
    return pltpu.CompilerParams(vmem_limit_bytes=size + 4 * 2**20)


def spaces():
    return (pl.BlockSpec(memory_space=s) for s in (pltpu.VMEM, pltpu.SMEM, pl.ANY))


def pick(table, query_refs, parts):
    height = table.shape[1] // parts
    row_of = iota((height, LANES), 0)
    lane_of = iota((LANES, LANES), 0)
    rows = jnp.concatenate([one_hot(row_of == (q >> 7)) for q in query_refs], axis=1)
    rows = jnp.concatenate([rows] * parts, axis=0) if parts > 1 else rows
    found = jnp.dot(table, rows, preferred_element_type=jnp.float32)
    return [
        (found[:, LANES * k : LANES * (k + 1)], lane_of == (q & (LANES - 1)))
        for k, q in enumerate(query_refs)
    ]


def lookup_body(first, last, planes_ref, query_ref, *refs):
    out_ref = refs[-1]
    count, group = planes_ref.shape[0] // LANES, 8
    if len(refs) > 1:
        out_ref[:first, :] = refs[0][:first, :]

    def step(i, carry):
        queries = [query_ref[pl.ds(group * i + k, 1), :] for k in range(group)]
        table = planes_ref[...]
        found = [
            pick(table[LANES * c : LANES * (c + 1)], queries, 1) for c in range(count)
        ]
        for k in range(group):
            total, hit = found[0][k]
            for c in range(1, count):
                total = total + found[c][k][0] * float(256**c)
            value = jnp.sum(jnp.where(hit, total, 0.0), axis=0, keepdims=True)
            out_ref[pl.ds(group * i + k, 1), :] = value.astype(jnp.int32)
        return carry

    lax.fori_loop(first // group, last // group, step, 0)


def planes_body(table_ref, out_ref):
    high = table_ref.shape[0]
    for c in range(out_ref.shape[0] // LANES):
        for h in range(0, high, LANES):
            byte = (table_ref[h : h + LANES, :] >> (8 * c)) & 255
            out_ref[LANES * c : LANES * (c + 1), h : h + LANES] = byte.astype(
                jnp.float32
            ).T.astype(jnp.bfloat16)


def byte_planes(table):
    size = table.shape[0]
    count = max(1, ((size - 1).bit_length() + 7) // 8)
    return pl.pallas_call(
        planes_body,
        out_shape=jax.ShapeDtypeStruct((count * LANES, size // LANES), jnp.bfloat16),
        compiler_params=room(table.size * 8),
        name="planes",
    )(table.reshape(-1, LANES))


def lookups(table, query):
    planes = byte_planes(table)
    rows = query.shape[0]
    edges = [0]
    for share in SHARES:
        edges.append(edges[-1] + rows // 16 // 8 * 8 * share)
    edges[-1] = rows
    found = ()
    for first, last in zip(edges, edges[1:]):
        found = (
            pl.pallas_call(
                functools.partial(lookup_body, first, last),
                out_shape=jax.ShapeDtypeStruct(query.shape, jnp.int32),
                compiler_params=room(planes.size * 16),
                name="lookup",
            )(planes, query, *found),
        )
    return found[0]


def pack_body(cum_ref, out_ref):
    half = out_ref.shape[0]
    rows = min(half, 64)

    def fixed(first):
        cum = cum_ref[pl.ds(first, rows), :]
        policy = (cum / jnp.sum(cum, axis=1, keepdims=True)).astype(jnp.bfloat16)
        return (policy.astype(jnp.float32) * float(2**SCALE_BITS) + 0.5).astype(jnp.int32)

    def step(i, carry):
        first = pl.multiple_of(i * rows, rows)
        out_ref[pl.ds(first, rows), :] = fixed(first) | (fixed(first + half) << 16)
        return carry

    lax.fori_loop(0, half // rows, step, 0, unroll=2)


def pack(opp_cum):
    rows, acts = opp_cum.shape
    return pl.pallas_call(
        pack_body,
        out_shape=jax.ShapeDtypeStruct((rows // 2, acts), jnp.int32),
        compiler_params=room(opp_cum.size * 6),
        name="pack",
    )(opp_cum)


def split(x, parts):
    out = []
    for _ in range(parts):
        out.append(x.astype(jnp.bfloat16))
        x = x - out[-1].astype(jnp.float32)
    return out


def outgoing(value_ref, row_ref, reach_ref, slot_ref, out_ref, weighted):
    table = jnp.concatenate(split(value_ref[...].T, 2), axis=1)
    group = 8

    def step(i, carry):
        queries = [row_ref[pl.ds(group * i + k, 1), :] for k in range(group)]
        for k, (found, hit) in enumerate(pick(table, queries, 2)):
            chosen = jnp.sum(jnp.where(hit, found, 0.0), axis=0, keepdims=True)
            weighted[pl.ds(group * i + k, 1), :] = chosen
        return carry

    lax.fori_loop(0, row_ref.shape[0] // group, step, 0)
    place = one_hot(iota((out_ref.shape[0], row_ref.shape[0]), 0) == slot_ref[...])
    total = jnp.zeros(out_ref.shape, jnp.float32)
    for part in split(weighted[...] * reach_ref[...], 3):
        total = total + jnp.dot(place, part, preferred_element_type=jnp.float32)
    out_ref[...] = total


def outgoing_rows(history_value, child_row, reach, slot, slots):
    return pl.pallas_call(
        outgoing,
        out_shape=jax.ShapeDtypeStruct((slots, LANES), jnp.float32),
        scratch_shapes=[pltpu.VMEM(child_row.shape, jnp.float32)],
        compiler_params=room(4 * 2**20),
        name="outgoing",
    )(history_value, child_row, reach, slot)


def value_body(blocks, place_ref, odd_ref, child_ref, row_ref, reach_ref, slot_ref, *rest):
    block_refs = rest[:blocks]
    value_ref, out_ref, table, weighted, sems = rest[blocks:]
    size = block_refs[0].shape[0]
    copies = [
        pltpu.make_async_copy(ref, table.at[pl.ds(8 + b * size, size), :], sems.at[b])
        for b, ref in enumerate(block_refs)
    ]
    for copy in copies:
        copy.start()
    for copy in copies:
        copy.wait()
    sub = iota((8, LANES), 0)
    spot = iota((8, LANES), 1) - sub

    tiles = value_ref.shape[0]

    def place(k, t):
        return place_ref.at[pl.ds(k * tiles, tiles)][t]

    def tile(t, carry):
        low = jnp.zeros((8, LANES), jnp.float32)
        high = jnp.zeros((8, LANES), jnp.float32)
        start = pl.multiple_of(t * LANES, LANES)
        children = child_ref.at[pl.ds(start, LANES), :]
        for g in range(LANES // 16):
            child = children[16 * g : 16 * g + 16, :].astype(jnp.float32)
            for half in range(2):
                at = 16 * g + 8 * half
                words = table[pl.ds(place(at, t) + 8, 8), :]
                for s in range(1, 8):
                    row = table[pl.ds(place(at + s, t) + (8 - s), 8), :]
                    words = jnp.where(sub == s, row, words)
                part = child[8 * half : 8 * half + 8]
                even = (words & 0xFFFF).astype(jnp.float32) * part
                odd = lax.shift_right_logical(words, 16).astype(jnp.float32) * part
                here = spot == at
                low = jnp.where(here, jnp.sum(even, axis=1, keepdims=True), low)
                high = jnp.where(here, jnp.sum(odd, axis=1, keepdims=True), high)
        low = jnp.sum(low, axis=0, keepdims=True)
        high = jnp.sum(high, axis=0, keepdims=True)
        picked = jnp.where(odd_ref[pl.ds(t, 1), :] > 0, high, low)
        value_ref[pl.ds(t, 1), :] = picked * (0.5**SCALE_BITS)
        return carry

    lax.fori_loop(0, tiles, tile, 0, unroll=2)
    outgoing(value_ref, row_ref, reach_ref, slot_ref, out_ref, weighted)


def values_from(blocks, place, odd, child_value, child_row, reach, slot, slots):
    size = blocks[0].shape[0]
    vmem, smem, hbm = spaces()
    return pl.pallas_call(
        functools.partial(value_body, len(blocks)),
        out_shape=(
            jax.ShapeDtypeStruct(odd.shape, jnp.float32),
            jax.ShapeDtypeStruct((slots, LANES), jnp.float32),
        ),
        in_specs=[smem] + [vmem] * 5 + [hbm] * len(blocks),
        out_specs=(vmem, vmem),
        scratch_shapes=[
            pltpu.VMEM((len(blocks) * size + 16, LANES), jnp.int32),
            pltpu.VMEM(child_row.shape, jnp.float32),
            pltpu.SemaphoreType.DMA((len(blocks),)),
        ],
        compiler_params=room(len(blocks) * size * LANES * 4 + 4 * 2**20),
        name="values",
    )(place.T.reshape(-1), odd, child_value, child_row, reach, slot, *blocks)


def regret_body(asked_ref, incoming_ref, cum_ref, gap_ref, total_ref):
    sets = cum_ref.shape[0]
    member = one_hot(iota((sets, asked_ref.shape[1]), 0) == asked_ref[...])
    value = jnp.zeros(cum_ref.shape, jnp.float32)
    for part in split(incoming_ref[...], 3):
        value = value + jnp.dot(member, part, preferred_element_type=jnp.float32)
    policy = cum_ref[...] / jnp.sum(cum_ref[...], axis=1, keepdims=True)
    gap = jnp.max(value, axis=1, keepdims=True) - jnp.sum(policy * value, axis=1, keepdims=True)
    own = iota((sets, LANES), 0) == iota((sets, LANES), 1)
    gap_ref[...] = jnp.sum(jnp.where(own, gap, 0.0), axis=0, keepdims=True)
    total = jnp.sum(jnp.broadcast_to(gap, (sets, LANES)), axis=0, keepdims=True)
    total_ref[...] = jnp.broadcast_to(total, total_ref.shape)


def regrets(asked, incoming, br_cum, devices):
    return pl.pallas_call(
        regret_body,
        out_shape=(
            jax.ShapeDtypeStruct((1, LANES), jnp.float32),
            jax.ShapeDtypeStruct((devices, LANES), jnp.float32),
        ),
        compiler_params=room(incoming.size * 16),
        name="regret",
    )(asked, incoming, br_cum)


def factors(n):
    high = 1
    while high * high < n:
        high *= 2
    return high, n // high


def exchange(block, across, depth, width):
    def device(y, core, z, x):
        return ((y * 2 + core) * depth + z) * width + x

    def move(array, to):
        pairs = []
        for y in range(across // 2):
            for core in range(2):
                for z in range(depth):
                    for x in range(width):
                        pairs.append((device(y, core, z, x), device(*to(y, core, z, x))))
        return lax.ppermute(array, AXES, pairs)

    def ring(y, core, z, x):
        return (y, core, (z + 1) % depth, x)

    def near(y, core, z, x):
        return (y, core, z, x ^ 1) if core == 0 else (y ^ 1, core, z, x)

    def far(y, core, z, x):
        return (y ^ 1, core, z, x) if core == 0 else (y, core, z, x ^ 1)

    def twin(y, core, z, x):
        return (y, 1 - core, z, x)

    start, beside, across_from, diagonal = [block], [], [], []
    for step in range(depth):
        if step:
            start.append(move(start[-1], ring))
        beside.append(move(start[-1], near))
        across_from.append(move(start[-1], far))
        if 0 < step < depth - 1:
            diagonal.append(move(diagonal[-1], ring))
        else:
            diagonal.append(move(beside[-1], far))
    mine = [part for group in zip(start, beside, across_from, diagonal) for part in group]
    return mine + [move(part, twin) for part in mine]


def local(child_value, child_row, opp_set, opp_home, opp_cum, reach, br_set, br_home, br_cum):
    across = lax.axis_size("gx")
    along = lax.axis_size("gy")
    devices = across * along
    depth, width = factors(along)
    hist, acts = child_value.shape
    parents = reach.shape[0]
    per_opp = opp_cum.shape[0]
    per_br = br_cum.shape[0]
    words = per_opp // 2
    limit_two = max(2, (2 * parents + devices - 1) // devices)

    packed = pack(opp_cum)

    home = lookups(opp_home, opp_set.reshape(hist // LANES, LANES))
    owner = home // per_opp
    inside = home % per_opp
    odd = inside // words
    home_two = jnp.take(br_home, br_set)
    owner_two = home_two // per_br
    earlier = jnp.arange(parents)[:, None] > jnp.arange(parents)[None, :]
    same = owner_two[:, None] == owner_two[None, :]
    rank_two = jnp.sum((earlier & same).astype(jnp.int32), axis=1)
    place_two = owner_two * limit_two + rank_two
    slots = devices * limit_two
    taken = place_two[None, :] == jnp.arange(slots, dtype=jnp.int32)[:, None]
    asked_two = jnp.sum(jnp.where(taken, home_two % per_br + 1, 0), axis=1) - 1
    early = jnp.concatenate(
        [
            asked_two.reshape(devices, limit_two).astype(jnp.float32),
            jnp.full((devices, 1), jnp.sum(reach)),
            jnp.zeros((devices, LANES - 1 - limit_two), jnp.float32),
        ],
        axis=1,
    )
    early = lax.all_to_all(early, AXES, split_axis=0, concat_axis=0, tiled=True)
    asked_two = early[:, :limit_two].astype(jnp.int32).reshape(-1)
    reach_total = jnp.sum(early[:, limit_two])

    rows_two = child_row.reshape(parents, acts)
    if across == 4 and (depth, width) == (4, 2) and devices * words * acts * 4 <= TABLE_LIMIT:
        gx, gy = lax.axis_index("gx"), lax.axis_index("gy")
        my_y, my_core, my_z, my_x = gx // 2, gx % 2, gy // width, gy % width
        y, core = owner // along // 2, owner // along % 2
        z, x = owner % along // width, owner % width
        flip_x, flip_y = x ^ my_x, y ^ my_y
        step = (my_z - z) % depth
        turn = jnp.where(core == 0, flip_x + 2 * flip_y, flip_y + 2 * flip_x)
        block = ((core ^ my_core) * depth + step) * 4 + turn
        place = block * words + inside % words
        blocks = exchange(packed, across, depth, width)
        history_value, outgoing_two = values_from(
            blocks, place, odd, child_value, rows_two, reach[:, None], place_two[None, :], slots
        )
    else:
        table = lax.all_gather(packed, AXES, axis=0, tiled=True)
        rows = jnp.take(table, (owner * words + inside % words).reshape(-1), axis=0)
        rows = lax.shift_right_logical(rows, 16 * odd.reshape(-1, 1)) & 0xFFFF
        history_value = jnp.einsum(
            "ra,ra->r", rows.astype(jnp.float32), child_value.astype(jnp.float32)
        ) * (0.5**SCALE_BITS)
        history_value = history_value.reshape(hist // LANES, LANES)
        outgoing_two = outgoing_rows(
            history_value, rows_two, reach[:, None], place_two[None, :], slots
        )
    incoming_two = lax.all_to_all(outgoing_two, AXES, split_axis=0, concat_axis=0, tiled=True)
    gap_row, gaps = regrets(asked_two[None, :], incoming_two, br_cum, devices)
    regret_gap = gap_row[0, :per_br]
    gaps = lax.all_to_all(gaps, AXES, split_axis=0, concat_axis=0, tiled=True)
    gap_total = jnp.sum(gaps[:, 0])
    return (history_value.reshape(-1), regret_gap, gap_total / reach_total)


def shortcut(mesh):
    gx, gy = mesh.shape["gx"], mesh.shape["gy"]
    return gx == 4 and factors(gy) == (4, 2)


def solution(mesh):
    placed = (
        P(AXES, None),
        P(AXES, None),
        P(AXES),
        P(),
        P(AXES, None),
        P(AXES),
        P(AXES),
        P(),
        P(AXES, None),
    )
    step = jax.shard_map(
        local,
        mesh=mesh,
        in_specs=placed,
        out_specs=(P(AXES), P(AXES), P()),
        check_vma=False,
    )
    return step if shortcut(mesh) else step
```

profile of v0, /device:TPU:0, one launch (start us, length us, event | category | flops | bytes accessed | tf_op | source)
XLA Modules:
  0.0 167.9 jit_solution(1289426103775887833)
XLA Ops:
  2.9 3.1 %collective-permute-start.3 = (s32[1024,128]{1,0:T(8,128)S(1)}, s32[1024,128]{1,0:T(8,128)S(1)}, u32[]{:S(2)}, u32[]{:S(2)}) collective-permute-start(s32[1024,128]{1,0:T(8,128)S(1)} %pack.1.rest_0_), channel_id=1, source_target_pairs={{0,2},{1,3},{2,4},{3,5},{4,6},{5,7},{6,0},{7,1},{8,10},{9,11},{10,... | collective-permute-start | bytes 1572872 | tf_op jit(solution)/shard_map/ppermute | solution.py:289
  6.0 1.5 collective-permute-start
  7.5 1.5 collective-permute-start.1
  9.0 10.9 %collective-permute-done.3.rest_4_ = s32[1024,128]{1,0:T(8,128)S(1)} collective-permute-done((s32[1024,128]{1,0:T(8,128)S(1)}, s32[1024,128]{1,0:T(8,128)S(1)}, u32[]{:S(2)}, u32[]{:S(2)}) %collective-permute-start.3) | collective-permute-done | bytes 524320 | tf_op jit(solution)/shard_map/ppermute | solution.py:289
  21.5 1.5 collective-permute-start.4
  24.2 10.7 %collective-permute-done.7.rest_8_ = s32[1024,128]{1,0:T(8,128)S(1)} collective-permute-done((s32[1024,128]{1,0:T(8,128)S(1)}, s32[1024,128]{1,0:T(8,128)S(1)}, u32[]{:S(2)}, u32[]{:S(2)}) %collective-permute-start.7) | collective-permute-done | bytes 524320 | tf_op jit(solution)/shard_map/ppermute | solution.py:289
  37.7 2.1 %collective-permute-done.5.rest_6_ = s32[1024,128]{1,0:T(8,128)} collective-permute-done((s32[1024,128]{1,0:T(8,128)S(1)}, s32[1024,128]{1,0:T(8,128)}, u32[]{:S(2)}, u32[]{:S(2)}) %collective-permute-start.5) | collective-permute-done | bytes 524320 | tf_op jit(solution)/shard_map/ppermute | solution.py:289
  41.3 1.3 collective-permute-start.9
  45.2 7.6 %collective-permute-done.11.rest_12_ = s32[1024,128]{1,0:T(8,128)} collective-permute-done((s32[1024,128]{1,0:T(8,128)S(1)}, s32[1024,128]{1,0:T(8,128)}, u32[]{:S(2)}, u32[]{:S(2)}) %collective-permute-start.11) | collective-permute-done | bytes 524320 | tf_op jit(solution)/shard_map/ppermute | solution.py:289
  52.8 1.7 %collective-permute-done.8.rest_9_ = s32[1024,128]{1,0:T(8,128)S(1)} collective-permute-done((s32[1024,128]{1,0:T(8,128)S(1)}, s32[1024,128]{1,0:T(8,128)S(1)}, u32[]{:S(2)}, u32[]{:S(2)}) %collective-permute-start.8) | collective-permute-done | bytes 524320 | tf_op jit(solution)/shard_map/ppermute | solution.py:289
  56.2 6.1 %collective-permute-done.6.rest_7_ = s32[1024,128]{1,0:T(8,128)S(1)} collective-permute-done((s32[1024,128]{1,0:T(8,128)}, s32[1024,128]{1,0:T(8,128)S(1)}, u32[]{:S(2)}, u32[]{:S(2)}) %collective-permute-start.6) | collective-permute-done | bytes 524320 | tf_op jit(solution)/shard_map/ppermute | solution.py:289
  67.6 2.0 %collective-permute-start.10 = (s32[1024,128]{1,0:T(8,128)}, s32[1024,128]{1,0:T(8,128)}, u32[]{:S(2)}, u32[]{:S(2)}) collective-permute-start(s32[1024,128]{1,0:T(8,128)} %copy-done.17), channel_id=1, source_target_pairs={{0,2},{1,3},{2,4},{3,5},{4,6},{5,7},{6,0},{7,1},{8,10},{9,11},{10,... | collective-permute-start | bytes 1572872 | tf_op jit(solution)/shard_map/ppermute | solution.py:289
  69.6 3.0 %collective-permute-done.13.rest_14_ = s32[1024,128]{1,0:T(8,128)} collective-permute-done((s32[1024,128]{1,0:T(8,128)}, s32[1024,128]{1,0:T(8,128)}, u32[]{:S(2)}, u32[]{:S(2)}) %collective-permute-start.13) | collective-permute-done | bytes 524320 | tf_op jit(solution)/shard_map/ppermute | solution.py:289
  77.8 6.1 %collective-permute-done.10.rest_11_ = s32[1024,128]{1,0:T(8,128)} collective-permute-done((s32[1024,128]{1,0:T(8,128)}, s32[1024,128]{1,0:T(8,128)}, u32[]{:S(2)}, u32[]{:S(2)}) %collective-permute-start.10) | collective-permute-done | bytes 524320 | tf_op jit(solution)/shard_map/ppermute | solution.py:289
  87.2 2.5 %all-to-all-start = ((f32[32,1,128]{2,1,0:T(1,128)}), f32[32,1,128]{2,1,0:T(1,128)S(1)}, u32[]{:S(2)}, u32[]{:S(2)}) async-start(f32[32,1,128]{2,1,0:T(1,128)} %bitcast.8), calls=%async_computation | async-start | bytes 32768 | tf_op jit(solution)/shard_map/all_to_all | solution.py:352
  91.7 2.9 %lookup.5.refs_0_ = s32[128,128]{1,0:T(8,128)S(1)} custom-call(bf16[256,512]{1,0:T(8,128)(2,1)S(1)} %planes.1.planes_ref, s32[128,128]{1,0:T(8,128)S(1)} %bitcast.20), custom_call_target="tpu_custom_call" | custom-call | tf_op jit(solution)/shard_map/lookup/pallas_call | solution.py:101
  95.4 1.7 %lookup.6.refs_0_ = s32[128,128]{1,0:T(8,128)S(1)} custom-call(bf16[256,512]{1,0:T(8,128)(2,1)S(1)} %planes.1.planes_ref, s32[128,128]{1,0:T(8,128)S(1)} %bitcast.21, s32[128,128]{1,0:T(8,128)S(1)} %lookup.5.refs_0_), custom_call_target="tpu_custom_call" | custom-call | tf_op jit(solution)/shard_map/lookup/pallas_call | solution.py:101
  97.1 3.5 %lookup.7.refs_0_ = s32[128,128]{1,0:T(8,128)S(1)} custom-call(bf16[256,512]{1,0:T(8,128)(2,1)S(1)} %planes.1.planes_ref, s32[128,128]{1,0:T(8,128)S(1)} %bitcast.22, s32[128,128]{1,0:T(8,128)S(1)} %lookup.6.refs_0_), custom_call_target="tpu_custom_call" | custom-call | tf_op jit(solution)/shard_map/lookup/pallas_call | solution.py:101
  102.4 2.2 %copy-done.1 = bf16[16384,128]{1,0:T(8,128)(2,1)S(1)} copy-done((bf16[16384,128]{1,0:T(8,128)(2,1)S(1)}, bf16[16384,128]{1,0:T(8,128)(2,1)}, u32[]{:S(2)}) %copy-start.1) | copy-done | bytes 4194328
  115.0 25.6 %values.1 = (f32[128,128]{1,0:T(8,128)}, f32[256,128]{1,0:T(8,128)}) custom-call(s32[16384]{0:T(1024)S(1)} %bitcast.26, s32[128,128]{1,0:T(8,128)S(1)} %get-tuple-element.13.odd_ref, bf16[16384,128]{1,0:T(8,128)(2,1)S(1)} %copy-done.1, s32[128,128]{1,0:T(8,128)S(1)} %bitcast.28, f32[128,1]{1,0:T(8,128)S(1)} %copy.19.reach_ref, s32[1,128]{1,0:T(1,128)S(1)} %bitcast.29, ...), custom_call_target="tpu_custom_call" | custom-call | tf_op jit(solution)/shard_map/values/pallas_call | solution.py:227
  140.6 5.8 %all-to-all-start.1 = ((f32[32,8,128]{2,1,0:T(8,128)}), f32[32,8,128]{2,1,0:T(8,128)S(1)}, u32[]{:S(2)}, u32[]{:S(2)}) async-start(f32[32,8,128]{2,1,0:T(8,128)} %bitcast.10), calls=%async_computation.1 | async-start | bytes 262144 | tf_op jit(solution)/shard_map/all_to_all | solution.py:382
  147.3 7.0 %all-to-all-done.1 = f32[32,8,128]{2,1,0:T(8,128)S(1)} async-done(((f32[32,8,128]{2,1,0:T(8,128)}), f32[32,8,128]{2,1,0:T(8,128)S(1)}, u32[]{:S(2)}, u32[]{:S(2)}) %all-to-all-start.1) | async-done | bytes 131104 | tf_op jit(solution)/shard_map/all_to_all | solution.py:382
  155.1 2.5 %all-to-all-start.2 = ((f32[32,1,128]{2,1,0:T(1,128)}), f32[32,1,128]{2,1,0:T(1,128)S(1)}, u32[]{:S(2)}, u32[]{:S(2)}) async-start(f32[32,1,128]{2,1,0:T(1,128)} %bitcast.14), calls=%async_computation.2 | async-start | bytes 32768 | tf_op jit(solution)/shard_map/all_to_all | solution.py:385
  158.2 6.6 %all-to-all-done.2 = f32[32,1,128]{2,1,0:T(1,128)S(1)} async-done(((f32[32,1,128]{2,1,0:T(1,128)}), f32[32,1,128]{2,1,0:T(1,128)S(1)}, u32[]{:S(2)}, u32[]{:S(2)}) %all-to-all-start.2) | async-done | bytes 16416 | tf_op jit(solution)/shard_map/all_to_all | solution.py:385
  (134 shorter events, 45.0 us)
Async XLA Ops:
  2.9 17.1 %collective-permute-start.3 = (s32[1024,128]{1,0:T(8,128)S(1)}, s32[1024,128]{1,0:T(8,128)S(1)}, u32[]{:S(2)}, u32[]{:S(2)}) collective-permute-start(s32[1024,128]{1,0:T(8,128)S(1)} %pack.1.rest_0_), channel_id=1, source_target_pairs={{0,2},{1,3},{2,4},{3,5},{4,6},{5,7},{6,0},{7,1},{8,10},{9,11},{10,... | collective-permute-start | bytes 1572872 | tf_op jit(solution)/shard_map/ppermute | solution.py:289
  6.0 14.6 %collective-permute-start = (s32[1024,128]{1,0:T(8,128)S(1)}, s32[1024,128]{1,0:T(8,128)S(1)}, u32[]{:S(2)}, u32[]{:S(2)}) collective-permute-start(s32[1024,128]{1,0:T(8,128)S(1)} %pack.1.rest_0_), channel_id=1, source_target_pairs={{0,1},{1,0},{2,3},{3,2},{4,5},{5,4},{6,7},{7,6},{8,24},{9,25},{10,... | collective-permute-start | bytes 1572872 | tf_op jit(solution)/shard_map/ppermute | solution.py:289
  7.5 15.5 %collective-permute-start.1 = (s32[1024,128]{1,0:T(8,128)S(1)}, s32[1024,128]{1,0:T(8,128)S(1)}, u32[]{:S(2)}, u32[]{:S(2)}) collective-permute-start(s32[1024,128]{1,0:T(8,128)S(1)} %pack.1.rest_0_), channel_id=1, source_target_pairs={{0,16},{1,17},{2,18},{3,19},{4,20},{5,21},{6,22},{7,23},{8,9},{9,8... | collective-permute-start | bytes 1572872 | tf_op jit(solution)/shard_map/ppermute | solution.py:289
  9.0 15.1 %collective-permute-start.15 = (s32[1024,128]{1,0:T(8,128)S(1)}, s32[1024,128]{1,0:T(8,128)S(1)}, u32[]{:S(2)}, u32[]{:S(2)}) collective-permute-start(s32[1024,128]{1,0:T(8,128)S(1)} %pack.1.rest_0_), channel_id=1, source_target_pairs={{0,8},{1,9},{2,10},{3,11},{4,12},{5,13},{6,14},{7,15},{8,0},{9,1},... | collective-permute-start | bytes 1572872 | tf_op jit(solution)/shard_map/ppermute | solution.py:289
  19.9 14.9 %collective-permute-start.7 = (s32[1024,128]{1,0:T(8,128)S(1)}, s32[1024,128]{1,0:T(8,128)S(1)}, u32[]{:S(2)}, u32[]{:S(2)}) collective-permute-start(s32[1024,128]{1,0:T(8,128)S(1)} %collective-permute-done.3.rest_4_), channel_id=1, source_target_pairs={{0,2},{1,3},{2,4},{3,5},{4,6},{5,7},{6,0},{7,1},{8,10},{9,11},{10,... | collective-permute-start | bytes 1572872 | tf_op jit(solution)/shard_map/ppermute | solution.py:289
  20.6 14.2 %collective-permute-start.2 = (s32[1024,128]{1,0:T(8,128)S(1)}, s32[1024,128]{1,0:T(8,128)}, u32[]{:S(2)}, u32[]{:S(2)}) collective-permute-start(s32[1024,128]{1,0:T(8,128)S(1)} %collective-permute-done.rest_1_), channel_id=1, source_target_pairs={{0,16},{1,17},{2,18},{3,19},{4,20},{5,21},{6,22},{7,23},{8,9},{9,8... | collective-permute-start | bytes 1572872 | tf_op jit(solution)/shard_map/ppermute | solution.py:289
  21.5 14.9 %collective-permute-start.4 = (s32[1024,128]{1,0:T(8,128)S(1)}, s32[1024,128]{1,0:T(8,128)}, u32[]{:S(2)}, u32[]{:S(2)}) collective-permute-start(s32[1024,128]{1,0:T(8,128)S(1)} %collective-permute-done.3.rest_4_), channel_id=1, source_target_pairs={{0,1},{1,0},{2,3},{3,2},{4,5},{5,4},{6,7},{7,6},{8,24},{9,25},{10,... | collective-permute-start | bytes 1572872 | tf_op jit(solution)/shard_map/ppermute | solution.py:289
  23.0 16.8 %collective-permute-start.5 = (s32[1024,128]{1,0:T(8,128)S(1)}, s32[1024,128]{1,0:T(8,128)}, u32[]{:S(2)}, u32[]{:S(2)}) collective-permute-start(s32[1024,128]{1,0:T(8,128)S(1)} %collective-permute-done.3.rest_4_), channel_id=1, source_target_pairs={{0,16},{1,17},{2,18},{3,19},{4,20},{5,21},{6,22},{7,23},{8,9},{9,8... | collective-permute-start | bytes 1572872 | tf_op jit(solution)/shard_map/ppermute | solution.py:289
  24.1 16.4 %collective-permute-start.19 = (s32[1024,128]{1,0:T(8,128)S(1)}, s32[1024,128]{1,0:T(8,128)S(1)}, u32[]{:S(2)}, u32[]{:S(2)}) collective-permute-start(s32[1024,128]{1,0:T(8,128)S(1)} %collective-permute-done.3.rest_4_), channel_id=1, source_target_pairs={{0,8},{1,9},{2,10},{3,11},{4,12},{5,13},{6,14},{7,15},{8,0},{9,1},... | collective-permute-start | bytes 1572872 | tf_op jit(solution)/shard_map/ppermute | solution.py:289
  36.4 16.4 %collective-permute-start.11 = (s32[1024,128]{1,0:T(8,128)S(1)}, s32[1024,128]{1,0:T(8,128)}, u32[]{:S(2)}, u32[]{:S(2)}) collective-permute-start(s32[1024,128]{1,0:T(8,128)S(1)} %collective-permute-done.7.rest_8_), channel_id=1, source_target_pairs={{0,2},{1,3},{2,4},{3,5},{4,6},{5,7},{6,0},{7,1},{8,10},{9,11},{10,... | collective-permute-start | bytes 1572872 | tf_op jit(solution)/shard_map/ppermute | solution.py:289
  39.8 14.8 %collective-permute-start.8 = (s32[1024,128]{1,0:T(8,128)S(1)}, s32[1024,128]{1,0:T(8,128)S(1)}, u32[]{:S(2)}, u32[]{:S(2)}) collective-permute-start(s32[1024,128]{1,0:T(8,128)S(1)} %collective-permute-done.7.rest_8_), channel_id=1, source_target_pairs={{0,1},{1,0},{2,3},{3,2},{4,5},{5,4},{6,7},{7,6},{8,24},{9,25},{10,... | collective-permute-start | bytes 1572872 | tf_op jit(solution)/shard_map/ppermute | solution.py:289
  41.3 13.2 %collective-permute-start.9 = (s32[1024,128]{1,0:T(8,128)S(1)}, s32[1024,128]{1,0:T(8,128)S(1)}, u32[]{:S(2)}, u32[]{:S(2)}) collective-permute-start(s32[1024,128]{1,0:T(8,128)S(1)} %collective-permute-done.7.rest_8_), channel_id=1, source_target_pairs={{0,16},{1,17},{2,18},{3,19},{4,20},{5,21},{6,22},{7,23},{8,9},{9,8... | collective-permute-start | bytes 1572872 | tf_op jit(solution)/shard_map/ppermute | solution.py:289
  44.3 18.0 %collective-permute-start.6 = (s32[1024,128]{1,0:T(8,128)}, s32[1024,128]{1,0:T(8,128)S(1)}, u32[]{:S(2)}, u32[]{:S(2)}) collective-permute-start(s32[1024,128]{1,0:T(8,128)} %collective-permute-done.2.rest_3_), channel_id=1, source_target_pairs={{0,2},{1,3},{2,4},{3,5},{4,6},{5,7},{6,0},{7,1},{8,10},{9,11},{10,... | collective-permute-start | bytes 1572872 | tf_op jit(solution)/shard_map/ppermute | solution.py:289
  52.8 14.7 %collective-permute-start.18 = (s32[1024,128]{1,0:T(8,128)}, s32[1024,128]{1,0:T(8,128)}, u32[]{:S(2)}, u32[]{:S(2)}) collective-permute-start(s32[1024,128]{1,0:T(8,128)} %collective-permute-done.2.rest_3_), channel_id=1, source_target_pairs={{0,8},{1,9},{2,10},{3,11},{4,12},{5,13},{6,14},{7,15},{8,0},{9,1},... | collective-permute-start | bytes 1572872 | tf_op jit(solution)/shard_map/ppermute | solution.py:289
  54.6 12.3 %collective-permute-start.20 = (s32[1024,128]{1,0:T(8,128)}, s32[1024,128]{1,0:T(8,128)}, u32[]{:S(2)}, u32[]{:S(2)}) collective-permute-start(s32[1024,128]{1,0:T(8,128)} %collective-permute-done.4.rest_5_), channel_id=1, source_target_pairs={{0,8},{1,9},{2,10},{3,11},{4,12},{5,13},{6,14},{7,15},{8,0},{9,1},... | collective-permute-start | bytes 1572872 | tf_op jit(solution)/shard_map/ppermute | solution.py:289
  54.6 12.4 %collective-permute-start.21 = (s32[1024,128]{1,0:T(8,128)}, s32[1024,128]{1,0:T(8,128)}, u32[]{:S(2)}, u32[]{:S(2)}) collective-permute-start(s32[1024,128]{1,0:T(8,128)} %collective-permute-done.5.rest_6_), channel_id=1, source_target_pairs={{0,8},{1,9},{2,10},{3,11},{4,12},{5,13},{6,14},{7,15},{8,0},{9,1},... | collective-permute-start | bytes 1572872 | tf_op jit(solution)/shard_map/ppermute | solution.py:289
  67.6 16.4 %collective-permute-start.10 = (s32[1024,128]{1,0:T(8,128)}, s32[1024,128]{1,0:T(8,128)}, u32[]{:S(2)}, u32[]{:S(2)}) collective-permute-start(s32[1024,128]{1,0:T(8,128)} %copy-done.17), channel_id=1, source_target_pairs={{0,2},{1,3},{2,4},{3,5},{4,6},{5,7},{6,0},{7,1},{8,10},{9,11},{10,... | collective-permute-start | bytes 1572872 | tf_op jit(solution)/shard_map/ppermute | solution.py:289
  75.7 26.6 %collective-permute-start.22 = (s32[1024,128]{1,0:T(8,128)}, s32[1024,128]{1,0:T(8,128)}, u32[]{:S(2)}, u32[]{:S(2)}) collective-permute-start(s32[1024,128]{1,0:T(8,128)} %copy-done.17), channel_id=1, source_target_pairs={{0,8},{1,9},{2,10},{3,11},{4,12},{5,13},{6,14},{7,15},{8,0},{9,1},... | collective-permute-start | bytes 1572872 | tf_op jit(solution)/shard_map/ppermute | solution.py:289
  76.5 25.9 %collective-permute-start.28 = (s32[1024,128]{1,0:T(8,128)}, s32[1024,128]{1,0:T(8,128)}, u32[]{:S(2)}, u32[]{:S(2)}) collective-permute-start(s32[1024,128]{1,0:T(8,128)} %collective-permute-done.12.rest_13_), channel_id=1, source_target_pairs={{0,8},{1,9},{2,10},{3,11},{4,12},{5,13},{6,14},{7,15},{8,0},{9,1},... | collective-permute-start | bytes 1572872 | tf_op jit(solution)/shard_map/ppermute | solution.py:289
  77.8 24.5 %collective-permute-start.29 = (s32[1024,128]{1,0:T(8,128)}, s32[1024,128]{1,0:T(8,128)}, u32[]{:S(2)}, u32[]{:S(2)}) collective-permute-start(s32[1024,128]{1,0:T(8,128)} %collective-permute-done.13.rest_14_), channel_id=1, source_target_pairs={{0,8},{1,9},{2,10},{3,11},{4,12},{5,13},{6,14},{7,15},{8,0},{9,1},... | collective-permute-start | bytes 1572872 | tf_op jit(solution)/shard_map/ppermute | solution.py:289
  83.9 18.5 %collective-permute-start.26 = (s32[1024,128]{1,0:T(8,128)}, s32[1024,128]{1,0:T(8,128)}, u32[]{:S(2)}, u32[]{:S(2)}) collective-permute-start(s32[1024,128]{1,0:T(8,128)} %collective-permute-done.10.rest_11_), channel_id=1, source_target_pairs={{0,8},{1,9},{2,10},{3,11},{4,12},{5,13},{6,14},{7,15},{8,0},{9,1},... | collective-permute-start | bytes 1572872 | tf_op jit(solution)/shard_map/ppermute | solution.py:289
  83.9 18.5 %collective-permute-start.30 = (s32[1024,128]{1,0:T(8,128)}, s32[1024,128]{1,0:T(8,128)}, u32[]{:S(2)}, u32[]{:S(2)}) collective-permute-start(s32[1024,128]{1,0:T(8,128)} %collective-permute-done.14.rest_15_), channel_id=1, source_target_pairs={{0,8},{1,9},{2,10},{3,11},{4,12},{5,13},{6,14},{7,15},{8,0},{9,1},... | collective-permute-start | bytes 1572872 | tf_op jit(solution)/shard_map/ppermute | solution.py:289
  87.2 53.4 %all-to-all-start = ((f32[32,1,128]{2,1,0:T(1,128)}), f32[32,1,128]{2,1,0:T(1,128)S(1)}, u32[]{:S(2)}, u32[]{:S(2)}) async-start(f32[32,1,128]{2,1,0:T(1,128)} %bitcast.8), calls=%async_computation | async-start | bytes 32768 | tf_op jit(solution)/shard_map/all_to_all | solution.py:352
  140.6 13.6 %all-to-all-start.1 = ((f32[32,8,128]{2,1,0:T(8,128)}), f32[32,8,128]{2,1,0:T(8,128)S(1)}, u32[]{:S(2)}, u32[]{:S(2)}) async-start(f32[32,8,128]{2,1,0:T(8,128)} %bitcast.10), calls=%async_computation.1 | async-start | bytes 262144 | tf_op jit(solution)/shard_map/all_to_all | solution.py:382
  (39 other events, 426.2 us)
where the time goes:
time: 169 us; the launch traced here: 168 us
  waiting for transfers between devices  63.6 us (38%)
  Pallas kernels  36.8 us (22%)
  starting transfers between devices  32.1 us (19%)
  local copies, waits for them, and re-layouts  26 us (15%)
  other arithmetic  5.87 us (3%)
  between operations  3.51 us (2%)
    ppermute x31, waiting for transfers between devices, move(): return lax.ppermute(array, AXES, pairs)  50 us
    pallas_call x1, Pallas kernels, values_from(): pl.pallas_call(functools.partial(value_body, len(blocks)), out_shape=(jax...  25.6 us
    unnamed x58, local copies, waits for them, and re-layouts  23.2 us
    ppermute x31, starting transfers between devices, move(): return lax.ppermute(array, AXES, pairs)  21.3 us
    pallas_call x5, Pallas kernels, lookups(): pl.pallas_call(functools.partial(lookup_body, first, last), out_shape=jax...  9.2 us
    all_to_all x1, waiting for transfers between devices, local(): lax.all_to_all(outgoing_two, AXES, split_axis=0, concat_axis=0, tiled=True)  6.97 us
    all_to_all x1, waiting for transfers between devices, local(): gaps = lax.all_to_all(gaps, AXES, split_axis=0, concat_axis=0, tiled=True)  6.63 us
    all_to_all x1, starting transfers between devices, local(): lax.all_to_all(outgoing_two, AXES, split_axis=0, concat_axis=0, tiled=True)  5.81 us
  transfers between devices with their start and end apart: 34, of which 12 were waited for; matrix products, arithmetic and copies ran while one was open for 5% of the time, Pallas kernels for 21%

commit v1 on v0

--- a/solution.py
+++ b/solution.py
@@ -12,7 +12,10 @@
 LANES = 128
 SCALE_BITS = 17
 TABLE_LIMIT = 24 * 2**20
-SHARES = (5, 3, 6, 1, 1)
+CHUNKS = 8
+SHARES = (5, 5, 4, 1, 1)
+STAGED = tuple(i for i in range(16) if i not in (11, 14, 15))
+STAGED += tuple(16 + i for i in range(16) if i not in (7, 11, 13, 14, 15))
 
 
 def iota(shape, dim):
@@ -143,7 +146,7 @@
     return out
 
 
-def outgoing(value_ref, row_ref, reach_ref, slot_ref, out_ref, weighted):
+def outgoing(value_ref, row_ref, reach_ref, slot_ref, note_ref, out_ref, weighted):
     table = jnp.concatenate(split(value_ref[...].T, 2), axis=1)
     group = 8
 
@@ -155,40 +158,109 @@
         return carry
 
     lax.fori_loop(0, row_ref.shape[0] // group, step, 0)
-    place = one_hot(iota((out_ref.shape[0], row_ref.shape[0]), 0) == slot_ref[...])
-    total = jnp.zeros(out_ref.shape, jnp.float32)
-    for part in split(weighted[...] * reach_ref[...], 3):
+    devices, tall = note_ref.shape[0], out_ref.shape[1]
+    limit = tall // 2
+    place = one_hot(iota((devices * limit, row_ref.shape[0]), 0) == slot_ref[...])
+    total = jnp.zeros((devices * limit, LANES), jnp.float32)
+    for part in split(weighted[...] * column(reach_ref[...]), 3):
         total = total + jnp.dot(place, part, preferred_element_type=jnp.float32)
-    out_ref[...] = total
-
-
-def outgoing_rows(history_value, child_row, reach, slot, slots):
+    for d in range(devices):
+        out_ref[d, :limit, :] = total[limit * d : limit * (d + 1)]
+        out_ref[d, limit:, :] = jnp.broadcast_to(note_ref[d : d + 1, :], (limit, LANES))
+
+
+def outgoing_rows(history_value, child_row, reach, slot, notes, limit):
     return pl.pallas_call(
         outgoing,
-        out_shape=jax.ShapeDtypeStruct((slots, LANES), jnp.float32),
+        out_shape=jax.ShapeDtypeStruct((notes.shape[0], 2 * limit, LANES), jnp.float32),
         scratch_shapes=[pltpu.VMEM(child_row.shape, jnp.float32)],
         compiler_params=room(4 * 2**20),
         name="outgoing",
-    )(history_value, child_row, reach, slot)
-
-
-def value_body(blocks, place_ref, odd_ref, child_ref, row_ref, reach_ref, slot_ref, *rest):
-    block_refs = rest[:blocks]
-    value_ref, out_ref, table, weighted, sems = rest[blocks:]
-    size = block_refs[0].shape[0]
-    copies = [
-        pltpu.make_async_copy(ref, table.at[pl.ds(8 + b * size, size), :], sems.at[b])
-        for b, ref in enumerate(block_refs)
+    )(history_value, child_row, reach, slot, notes)
+
+
+def fill(refs, slots, table, sems):
+    size = refs[0].shape[0]
+    return [
+        pltpu.make_async_copy(ref, table.at[pl.ds(8 + b * size, size), :], sems.at[i])
+        for i, (ref, b) in enumerate(zip(refs, slots))
     ]
+
+
+def quotient(x, n):
+    return x >> (n.bit_length() - 1) if n & (n - 1) == 0 else x // n
+
+
+def split_by(x, n):
+    whole = quotient(x, n)
+    return whole, x - whole * n
+
+
+def stage_body(slots, along, width, words, home_ref, *refs):
+    block_refs, (table, place_ref, odd_ref, sems) = refs[: len(slots)], refs[len(slots) :]
+    copies = fill(block_refs, slots, table, sems)
     for copy in copies:
         copy.start()
+    depth = along // width
+    gx, gy = lax.axis_index("gx"), lax.axis_index("gy")
+    my_y, my_core = split_by(gx, 2)
+    my_z, my_x = split_by(gy, width)
+    row, inside = split_by(home_ref[...], words)
+    owner, odd = split_by(row, 2)
+    chip, place = split_by(owner, along)
+    y, core = split_by(chip, 2)
+    z, x = split_by(place, width)
+    flip_x, flip_y = x ^ my_x, y ^ my_y
+    turn = jnp.where(core == 0, flip_x + 2 * flip_y, flip_y + 2 * flip_x)
+    step = my_z - z
+    step = jnp.where(step < 0, step + depth, step)
+    block = ((core ^ my_core) * depth + step) * 4 + turn
+    at = (block * words + inside).astype(jnp.float32)
+    place_ref[...] = at.T.astype(jnp.int32)
+    odd_ref[...] = odd
+    for copy in copies:
+        copy.wait()
+
+
+def staged(blocks, home, along, width):
+    size = blocks[0].shape[0]
+    vmem, _, hbm = spaces()
+    shape = (len(blocks) * size + 16, LANES)
+    return pl.pallas_call(
+        functools.partial(stage_body, STAGED, along, width, size),
+        out_shape=(
+            jax.ShapeDtypeStruct(shape, jnp.int32),
+            jax.ShapeDtypeStruct(home.shape[::-1], jnp.int32),
+            jax.ShapeDtypeStruct(home.shape, jnp.int32),
+        ),
+        in_specs=[vmem] + [hbm] * len(STAGED),
+        out_specs=(vmem, vmem, vmem),
+        scratch_shapes=[pltpu.SemaphoreType.DMA((len(STAGED),))],
+        compiler_params=room(0),
+        name="stage",
+    )(home, *(blocks[b] for b in STAGED))
+
+
+def value_body(slots, place_ref, odd_ref, child_ref, *rest):
+    upper, block_refs = rest[:4], rest[5 : 5 + len(slots)]
+    value_ref, out_ref, table, child, weighted, sems, arrived = rest[5 + len(slots) :]
+    copies = fill(block_refs, slots, table, sems)
+    tiles = value_ref.shape[0]
+    chunk = tiles // CHUNKS
+
+    def children_of(c):
+        rows = pl.ds(c * chunk * LANES, chunk * LANES)
+        return pltpu.make_async_copy(child_ref.at[rows, :], child.at[rows, :], arrived.at[c])
+
+    for copy in copies:
+        copy.start()
+    for c in range(CHUNKS):
+        children_of(c).start()
     for copy in copies:
         copy.wait()
     sub = iota((8, LANES), 0)
     spot = iota((8, LANES), 1) - sub
 
-    tiles = value_ref.shape[0]
-
     def place(k, t):
         return place_ref.at[pl.ds(k * tiles, tiles)][t]
 
@@ -196,16 +268,16 @@
         low = jnp.zeros((8, LANES), jnp.float32)
         high = jnp.zeros((8, LANES), jnp.float32)
         start = pl.multiple_of(t * LANES, LANES)
-        children = child_ref.at[pl.ds(start, LANES), :]
+        children = child.at[pl.ds(start, LANES), :]
         for g in range(LANES // 16):
-            child = children[16 * g : 16 * g + 16, :].astype(jnp.float32)
+            values = children[16 * g : 16 * g + 16, :].astype(jnp.float32)
             for half in range(2):
                 at = 16 * g + 8 * half
                 words = table[pl.ds(place(at, t) + 8, 8), :]
                 for s in range(1, 8):
                     row = table[pl.ds(place(at + s, t) + (8 - s), 8), :]
                     words = jnp.where(sub == s, row, words)
-                part = child[8 * half : 8 * half + 8]
+                part = values[8 * half : 8 * half + 8]
                 even = (words & 0xFFFF).astype(jnp.float32) * part
                 odd = lax.shift_right_logical(words, 16).astype(jnp.float32) * part
                 here = spot == at
@@ -217,55 +289,134 @@
         value_ref[pl.ds(t, 1), :] = picked * (0.5**SCALE_BITS)
         return carry
 
-    lax.fori_loop(0, tiles, tile, 0, unroll=2)
-    outgoing(value_ref, row_ref, reach_ref, slot_ref, out_ref, weighted)
-
-
-def values_from(blocks, place, odd, child_value, child_row, reach, slot, slots):
-    size = blocks[0].shape[0]
+    def stretch(c, carry):
+        children_of(c).wait()
+        return lax.fori_loop(
+            0, chunk, lambda i, carry: tile(c * chunk + i, carry), carry, unroll=4
+        )
+
+    lax.fori_loop(0, CHUNKS, stretch, 0)
+    outgoing(value_ref, *upper, out_ref, weighted)
+
+
+def values_from(blocks, home, along, width, child_value, child_row, reach, slot, notes, limit):
+    table, place, odd = staged(blocks, home, along, width)
+    rest = tuple(b for b in range(len(blocks)) if b not in STAGED)
     vmem, smem, hbm = spaces()
     return pl.pallas_call(
-        functools.partial(value_body, len(blocks)),
+        functools.partial(value_body, rest),
         out_shape=(
             jax.ShapeDtypeStruct(odd.shape, jnp.float32),
-            jax.ShapeDtypeStruct((slots, LANES), jnp.float32),
+            jax.ShapeDtypeStruct((notes.shape[0], 2 * limit, LANES), jnp.float32),
+            jax.ShapeDtypeStruct(table.shape, table.dtype),
         ),
-        in_specs=[smem] + [vmem] * 5 + [hbm] * len(blocks),
-        out_specs=(vmem, vmem),
+        in_specs=[smem, vmem, pl.BlockSpec(memory_space=pltpu.HBM)]
+        + [vmem] * 5
+        + [hbm] * len(rest),
+        out_specs=(vmem, vmem, vmem),
         scratch_shapes=[
-            pltpu.VMEM((len(blocks) * size + 16, LANES), jnp.int32),
+            pltpu.VMEM(child_value.shape, child_value.dtype),
             pltpu.VMEM(child_row.shape, jnp.float32),
-            pltpu.SemaphoreType.DMA((len(blocks),)),
+            pltpu.SemaphoreType.DMA((len(rest),)),
+            pltpu.SemaphoreType.DMA((CHUNKS,)),
         ],
-        compiler_params=room(len(blocks) * size * LANES * 4 + 4 * 2**20),
+        input_output_aliases={7: 2},
+        compiler_params=room(8 * 2**20),
         name="values",
-    )(place.T.reshape(-1), odd, child_value, child_row, reach, slot, *blocks)
-
-
-def regret_body(asked_ref, incoming_ref, cum_ref, gap_ref, total_ref):
+    )(
+        place.reshape(-1),
+        odd,
+        pltpu.with_memory_space_constraint(child_value, pltpu.HBM),
+        child_row,
+        reach,
+        slot,
+        notes,
+        table,
+        *(blocks[b] for b in rest),
+    )[:2]
+
+
+def column(row):
+    return jnp.broadcast_to(row.astype(jnp.float32), (row.shape[1], row.shape[1])).T
+
+
+def slots_body(per_br, limit, home_ref, set_ref, reach_ref, place_ref, note_ref):
+    parents = set_ref.shape[1]
+    count = max(1, ((home_ref.size - 1).bit_length() + 7) // 8)
+    home = jnp.zeros(set_ref.shape, jnp.float32)
+    for c in range(count):
+        byte = ((home_ref[...] >> (8 * c)) & 255).astype(jnp.float32)
+        ((found, hit),) = pick(byte.T.astype(jnp.bfloat16), [set_ref[...]], 1)
+        home += jnp.sum(jnp.where(hit, found, 0.0), axis=0, keepdims=True) * float(256**c)
+    home = home.astype(jnp.int32)
+    owner = quotient(home, per_br)
+    inside = home - owner * per_br
+    square = (parents, parents)
+    earlier = iota(square, 0) < iota(square, 1)
+    same = column(owner) == owner.astype(jnp.float32)
+    rank = jnp.sum(jnp.where(earlier & same, 1.0, 0.0), axis=0, keepdims=True)
+    place_ref[...] = owner * limit + rank.astype(jnp.int32)
+    devices = note_ref.shape[0]
+    here = iota((devices, parents), 0) == owner
+    rows = jnp.where(here, (inside + 1).astype(jnp.float32), 0.0).astype(jnp.bfloat16)
+    ranks = one_hot(column(rank) == iota((parents, LANES), 1).astype(jnp.float32))
+    asked = jnp.dot(rows, ranks, preferred_element_type=jnp.float32) - 1.0
+    reach = jnp.sum(jnp.broadcast_to(reach_ref[...], note_ref.shape), axis=1, keepdims=True)
+    note_ref[...] = jnp.where(iota(note_ref.shape, 1) == limit, reach, asked)
+
+
+def slots_of(br_home, br_set, reach, per_br, devices, limit):
+    return pl.pallas_call(
+        functools.partial(slots_body, per_br, limit),
+        out_shape=(
+            jax.ShapeDtypeStruct((1, br_set.shape[0]), jnp.int32),
+            jax.ShapeDtypeStruct((devices, LANES), jnp.float32),
+        ),
+        compiler_params=room(2**20),
+        name="slots",
+    )(br_home.reshape(-1, LANES), br_set[None, :], reach[None, :])
+
+
+def regret_body(incoming_ref, cum_ref, gap_ref, total_ref, reach_ref):
     sets = cum_ref.shape[0]
-    member = one_hot(iota((sets, asked_ref.shape[1]), 0) == asked_ref[...])
+    devices, limit = incoming_ref.shape[0], incoming_ref.shape[1] // 2
+    notes = jnp.concatenate([incoming_ref[d, limit : limit + 1, :] for d in range(devices)], axis=0)
+    lane = iota((devices, LANES), 1)
     value = jnp.zeros(cum_ref.shape, jnp.float32)
-    for part in split(incoming_ref[...], 3):
-        value = value + jnp.dot(member, part, preferred_element_type=jnp.float32)
+    rows = jnp.concatenate([incoming_ref[d, :limit, :] for d in range(devices)], axis=0)
+    spread = jnp.concatenate(
+        [jnp.broadcast_to(notes[d : d + 1, :], (limit, LANES)) for d in range(devices)], axis=0
+    )
+    mine = iota(spread.shape, 1) == iota(spread.shape, 0) % limit
+    asked = jnp.sum(jnp.where(mine, spread, 0.0), axis=1, keepdims=True)
+    wide = jnp.broadcast_to(asked, spread.shape)
+    member = one_hot(wide == iota(spread.shape, 1).astype(jnp.float32))
+    for part in split(rows, 3):
+        value = value + lax.dot_general(
+            member, part, (((0,), (0,)), ((), ())), preferred_element_type=jnp.float32
+        )[:sets]
     policy = cum_ref[...] / jnp.sum(cum_ref[...], axis=1, keepdims=True)
     gap = jnp.max(value, axis=1, keepdims=True) - jnp.sum(policy * value, axis=1, keepdims=True)
     own = iota((sets, LANES), 0) == iota((sets, LANES), 1)
     gap_ref[...] = jnp.sum(jnp.where(own, gap, 0.0), axis=0, keepdims=True)
     total = jnp.sum(jnp.broadcast_to(gap, (sets, LANES)), axis=0, keepdims=True)
     total_ref[...] = jnp.broadcast_to(total, total_ref.shape)
-
-
-def regrets(asked, incoming, br_cum, devices):
+    reach = jnp.sum(jnp.where(lane == limit, notes, 0.0), axis=1, keepdims=True)
+    reach = jnp.sum(jnp.broadcast_to(reach, notes.shape), axis=0, keepdims=True)
+    reach_ref[...] = reach
+
+
+def regrets(incoming, br_cum):
     return pl.pallas_call(
         regret_body,
         out_shape=(
             jax.ShapeDtypeStruct((1, LANES), jnp.float32),
-            jax.ShapeDtypeStruct((devices, LANES), jnp.float32),
+            jax.ShapeDtypeStruct((incoming.shape[0], LANES), jnp.float32),
+            jax.ShapeDtypeStruct((1, LANES), jnp.float32),
         ),
         compiler_params=room(incoming.size * 16),
         name="regret",
-    )(asked, incoming, br_cum)
+    )(incoming, br_cum)
 
 
 def factors(n):
@@ -300,17 +451,17 @@
     def twin(y, core, z, x):
         return (y, 1 - core, z, x)
 
-    start, beside, across_from, diagonal = [block], [], [], []
-    for step in range(depth):
-        if step:
+    start, beside, opposite, diagonal = [block], [], [], []
+    for i in range(depth):
+        if i:
             start.append(move(start[-1], ring))
         beside.append(move(start[-1], near))
-        across_from.append(move(start[-1], far))
-        if 0 < step < depth - 1:
+        opposite.append(move(start[-1], far))
+        if 0 < i < depth - 1:
             diagonal.append(move(diagonal[-1], ring))
         else:
             diagonal.append(move(beside[-1], far))
-    mine = [part for group in zip(start, beside, across_from, diagonal) for part in group]
+    mine = [part for group in zip(start, beside, opposite, diagonal) for part in group]
     return mine + [move(part, twin) for part in mine]
 
 
@@ -329,46 +480,16 @@
     packed = pack(opp_cum)
 
     home = lookups(opp_home, opp_set.reshape(hist // LANES, LANES))
-    owner = home // per_opp
-    inside = home % per_opp
-    odd = inside // words
-    home_two = jnp.take(br_home, br_set)
-    owner_two = home_two // per_br
-    earlier = jnp.arange(parents)[:, None] > jnp.arange(parents)[None, :]
-    same = owner_two[:, None] == owner_two[None, :]
-    rank_two = jnp.sum((earlier & same).astype(jnp.int32), axis=1)
-    place_two = owner_two * limit_two + rank_two
-    slots = devices * limit_two
-    taken = place_two[None, :] == jnp.arange(slots, dtype=jnp.int32)[:, None]
-    asked_two = jnp.sum(jnp.where(taken, home_two % per_br + 1, 0), axis=1) - 1
-    early = jnp.concatenate(
-        [
-            asked_two.reshape(devices, limit_two).astype(jnp.float32),
-            jnp.full((devices, 1), jnp.sum(reach)),
-            jnp.zeros((devices, LANES - 1 - limit_two), jnp.float32),
-        ],
-        axis=1,
-    )
-    early = lax.all_to_all(early, AXES, split_axis=0, concat_axis=0, tiled=True)
-    asked_two = early[:, :limit_two].astype(jnp.int32).reshape(-1)
-    reach_total = jnp.sum(early[:, limit_two])
-
+    place_two, notes = slots_of(br_home, br_set, reach, per_br, devices, limit_two)
     rows_two = child_row.reshape(parents, acts)
     if across == 4 and (depth, width) == (4, 2) and devices * words * acts * 4 <= TABLE_LIMIT:
-        gx, gy = lax.axis_index("gx"), lax.axis_index("gy")
-        my_y, my_core, my_z, my_x = gx // 2, gx % 2, gy // width, gy % width
-        y, core = owner // along // 2, owner // along % 2
-        z, x = owner % along // width, owner % width
-        flip_x, flip_y = x ^ my_x, y ^ my_y
-        step = (my_z - z) % depth
-        turn = jnp.where(core == 0, flip_x + 2 * flip_y, flip_y + 2 * flip_x)
-        block = ((core ^ my_core) * depth + step) * 4 + turn
-        place = block * words + inside % words
         blocks = exchange(packed, across, depth, width)
         history_value, outgoing_two = values_from(
-            blocks, place, odd, child_value, rows_two, reach[:, None], place_two[None, :], slots
+            blocks, home, along, width, child_value, rows_two, reach[None, :], place_two, notes, limit_two
         )
     else:
+        owner, inside = home // per_opp, home % per_opp
+        odd = inside // words
         table = lax.all_gather(packed, AXES, axis=0, tiled=True)
         rows = jnp.take(table, (owner * words + inside % words).reshape(-1), axis=0)
         rows = lax.shift_right_logical(rows, 16 * odd.reshape(-1, 1)) & 0xFFFF
@@ -377,14 +498,14 @@
         ) * (0.5**SCALE_BITS)
         history_value = history_value.reshape(hist // LANES, LANES)
         outgoing_two = outgoing_rows(
-            history_value, rows_two, reach[:, None], place_two[None, :], slots
+            history_value, rows_two, reach[None, :], place_two, notes, limit_two
         )
     incoming_two = lax.all_to_all(outgoing_two, AXES, split_axis=0, concat_axis=0, tiled=True)
-    gap_row, gaps = regrets(asked_two[None, :], incoming_two, br_cum, devices)
+    gap_row, gaps, reach_row = regrets(incoming_two, br_cum)
     regret_gap = gap_row[0, :per_br]
     gaps = lax.all_to_all(gaps, AXES, split_axis=0, concat_axis=0, tiled=True)
     gap_total = jnp.sum(gaps[:, 0])
-    return (history_value.reshape(-1), regret_gap, gap_total / reach_total)
+    return (history_value.reshape(-1), regret_gap, gap_total / reach_row[0, 0])
 
 
 def shortcut(mesh):

time: 169 us -> 150 us (0.89)
  local copies, waits for them, and re-layouts: 26 us -> 6.36 us
  blocking collectives: 0 us -> 13.1 us
  starting transfers between devices: 32.1 us -> 22.7 us
  waiting for transfers between devices: 63.6 us -> 71.1 us
  other arithmetic: 5.87 us -> 0.6 us
  Pallas kernels: 36.8 us -> 33.4 us
    unnamed x58 -> x20, local copies, waits for them, and re-layouts: 23.2 us -> 5.85 us
    ppermute x31, waiting for transfers between devices: 50 us -> 64.4 us  [move(): return lax.ppermute(array, AXES, pairs)]
    all_to_all x0 -> x1, blocking collectives: none -> 13.1 us  [local(): lax.all_to_all(outgoing_two, AXES, split_axis=0, concat_axis=0, tiled=True)]
    all_to_all x2 -> x0, starting transfers between devices: 8.32 us -> none  [the longest x1 5.81 us: local(): lax.all_to_all(outgoing_two, AXES, split_axis=0, concat_axis=0, tiled=True)]
    all_to_all x2 -> x0, waiting for transfers between devices: 6.97 us -> none  [the longest x1 6.97 us: local(): lax.all_to_all(outgoing_two, AXES, split_axis=0, concat_axis=0, tiled=True)]
    pallas_call x1 -> x3, Pallas kernels: 25.6 us -> 22 us  [the longest x1 20.2 us: values_from(): pl.pallas_call(functools.partial(value_body, rest), out_shape=(jax.ShapeD...]
    reduce_sum x4 -> x0, other arithmetic: 2.3 us -> none  [the longest x1 1.27 us: local(): jnp.sum(reach)]
  transfers between devices with their start and end apart: 34 -> 32, of which waited for: 12 -> 8; matrix products, arithmetic and copies ran while one was open for 5% -> 0% of each run, Pallas kernels for 21% -> 7%
where the time goes in v1:
time: 150 us
  waiting for transfers between devices  71.1 us (47%)
  Pallas kernels  33.4 us (22%)
  starting transfers between devices  22.7 us (15%)
  blocking collectives  13.1 us (9%)
  local copies, waits for them, and re-layouts  6.36 us (4%)
  between operations  2.69 us (2%)
    ppermute x31, waiting for transfers between devices, move(): return lax.ppermute(array, AXES, pairs)  64.4 us
    ppermute x31, starting transfers between devices, move(): return lax.ppermute(array, AXES, pairs)  20.2 us
    pallas_call x1, Pallas kernels, values_from(): pl.pallas_call(functools.partial(value_body, rest), out_shape=(jax.ShapeD...  20.2 us
    all_to_all x1, blocking collectives, local(): lax.all_to_all(outgoing_two, AXES, split_axis=0, concat_axis=0, tiled=True)  13.1 us
    pallas_call x5, Pallas kernels, lookups(): pl.pallas_call(functools.partial(lookup_body, first, last), out_shape=jax...  9.2 us
    all_to_all x1, waiting for transfers between devices, local(): gaps = lax.all_to_all(gaps, AXES, split_axis=0, concat_axis=0, tiled=True)  6.63 us
    unnamed x20, local copies, waits for them, and re-layouts  5.85 us
  transfers between devices with their start and end apart: 32, of which 8 were waited for; matrix products, arithmetic and copies ran while one was open for 0% of the time, Pallas kernels for 7%

profile of v1, /device:TPU:0, one launch (start us, length us, event | category | flops | bytes accessed | tf_op | source)
XLA Modules:
  0.0 149.9 jit_solution(17336911510844503989)
XLA Ops:
  2.9 3.1 %collective-permute-start.3 = (s32[1024,128]{1,0:T(8,128)S(1)}, s32[1024,128]{1,0:T(8,128)S(1)}, u32[]{:S(2)}, u32[]{:S(2)}) collective-permute-start(s32[1024,128]{1,0:T(8,128)S(1)} %pack.1.refs_0_), channel_id=1, source_target_pairs={{0,2},{1,3},{2,4},{3,5},{4,6},{5,7},{6,0},{7,1},{8,10},{9,11},{10,... | collective-permute-start | bytes 1572872 | tf_op jit(solution)/shard_map/ppermute | solution.py:440
  6.0 1.5 %collective-permute-start.1 = (s32[1024,128]{1,0:T(8,128)S(1)}, s32[1024,128]{1,0:T(8,128)S(1)}, u32[]{:S(2)}, u32[]{:S(2)}) collective-permute-start(s32[1024,128]{1,0:T(8,128)S(1)} %pack.1.refs_0_), channel_id=1, source_target_pairs={{0,16},{1,17},{2,18},{3,19},{4,20},{5,21},{6,22},{7,23},{8,9},{9,8... | collective-permute-start | bytes 1572872 | tf_op jit(solution)/shard_map/ppermute | solution.py:440
  7.5 1.5 collective-permute-start
  9.0 10.9 %collective-permute-done.3.refs_4_ = s32[1024,128]{1,0:T(8,128)S(1)} collective-permute-done((s32[1024,128]{1,0:T(8,128)S(1)}, s32[1024,128]{1,0:T(8,128)S(1)}, u32[]{:S(2)}, u32[]{:S(2)}) %collective-permute-start.3) | collective-permute-done | bytes 524320 | tf_op jit(solution)/shard_map/ppermute | solution.py:440
  19.9 1.6 %collective-permute-start.5 = (s32[1024,128]{1,0:T(8,128)S(1)}, s32[1024,128]{1,0:T(8,128)S(1)}, u32[]{:S(2)}, u32[]{:S(2)}) collective-permute-start(s32[1024,128]{1,0:T(8,128)S(1)} %collective-permute-done.3.refs_4_), channel_id=1, source_target_pairs={{0,16},{1,17},{2,18},{3,19},{4,20},{5,21},{6,22},{7,23},{8,9},{9,8... | collective-permute-start | bytes 1572872 | tf_op jit(solution)/shard_map/ppermute | solution.py:440
  21.5 1.5 collective-permute-start.4
  23.5 12.5 %collective-permute-done.7.refs_8_ = s32[1024,128]{1,0:T(8,128)S(1)} collective-permute-done((s32[1024,128]{1,0:T(8,128)S(1)}, s32[1024,128]{1,0:T(8,128)S(1)}, u32[]{:S(2)}, u32[]{:S(2)}) %collective-permute-start.7) | collective-permute-done | bytes 524320 | tf_op jit(solution)/shard_map/ppermute | solution.py:440
  36.1 1.5 %collective-permute-start.2 = (s32[1024,128]{1,0:T(8,128)S(1)}, s32[1024,128]{1,0:T(8,128)S(1)}, u32[]{:S(2)}, u32[]{:S(2)}) collective-permute-start(s32[1024,128]{1,0:T(8,128)S(1)} %collective-permute-done.refs_1_), channel_id=1, source_target_pairs={{0,16},{1,17},{2,18},{3,19},{4,20},{5,21},{6,22},{7,23},{8,9},{9,8... | collective-permute-start | bytes 1572872 | tf_op jit(solution)/shard_map/ppermute | solution.py:440
  39.7 8.8 %collective-permute-done.2.refs_3_ = s32[1024,128]{1,0:T(8,128)S(1)} collective-permute-done((s32[1024,128]{1,0:T(8,128)S(1)}, s32[1024,128]{1,0:T(8,128)S(1)}, u32[]{:S(2)}, u32[]{:S(2)}) %collective-permute-start.2) | collective-permute-done | bytes 524320 | tf_op jit(solution)/shard_map/ppermute | solution.py:440
  49.1 4.7 %collective-permute-done.10.refs_11_ = s32[1024,128]{1,0:T(8,128)S(1)} collective-permute-done((s32[1024,128]{1,0:T(8,128)S(1)}, s32[1024,128]{1,0:T(8,128)S(1)}, u32[]{:S(2)}, u32[]{:S(2)}) %collective-permute-start.10) | collective-permute-done | bytes 524320 | tf_op jit(solution)/shard_map/ppermute | solution.py:440
  53.7 2.7 %collective-permute-done.9.refs_10_ = s32[1024,128]{1,0:T(8,128)S(1)} collective-permute-done((s32[1024,128]{1,0:T(8,128)S(1)}, s32[1024,128]{1,0:T(8,128)S(1)}, u32[]{:S(2)}, u32[]{:S(2)}) %collective-permute-start.9) | collective-permute-done | bytes 524320 | tf_op jit(solution)/shard_map/ppermute | solution.py:440
  56.5 1.5 %collective-permute-start.24 = (s32[1024,128]{1,0:T(8,128)S(1)}, s32[1024,128]{1,0:T(8,128)S(1)}, u32[]{:S(2)}, u32[]{:S(2)}) collective-permute-start(s32[1024,128]{1,0:T(8,128)S(1)} %collective-permute-done.10.refs_11_), channel_id=1, source_target_pairs={{0,16},{1,17},{2,18},{3,19},{4,20},{5,21},{6,22},{7,23},{8,9},{9,8... | collective-permute-start | bytes 1572872 | tf_op jit(solution)/shard_map/ppermute | solution.py:440
  58.0 1.5 collective-permute-start.11
  60.0 10.9 %collective-permute-done.6.refs_7_ = s32[1024,128]{1,0:T(8,128)S(1)} collective-permute-done((s32[1024,128]{1,0:T(8,128)S(1)}, s32[1024,128]{1,0:T(8,128)S(1)}, u32[]{:S(2)}, u32[]{:S(2)}) %collective-permute-start.6) | collective-permute-done | bytes 524320 | tf_op jit(solution)/shard_map/ppermute | solution.py:440
  70.9 1.6 %collective-permute-start.25 = (s32[1024,128]{1,0:T(8,128)S(1)}, s32[1024,128]{1,0:T(8,128)S(1)}, u32[]{:S(2)}, u32[]{:S(2)}) collective-permute-start(s32[1024,128]{1,0:T(8,128)S(1)} %collective-permute-done.11.refs_12_), channel_id=1, source_target_pairs={{0,16},{1,17},{2,18},{3,19},{4,20},{5,21},{6,22},{7,23},{8,9},{9,8... | collective-permute-start | bytes 1572872 | tf_op jit(solution)/shard_map/ppermute | solution.py:440
  73.2 13.8 %collective-permute-done.23.rest_5_ = s32[1024,128]{1,0:T(8,128)S(1)} collective-permute-done((s32[1024,128]{1,0:T(8,128)S(1)}, s32[1024,128]{1,0:T(8,128)S(1)}, u32[]{:S(2)}, u32[]{:S(2)}) %collective-permute-start.23) | collective-permute-done | bytes 524320 | tf_op jit(solution)/shard_map/ppermute | solution.py:440
  89.5 2.9 %lookup.5.refs_0_ = s32[128,128]{1,0:T(8,128)S(1)} custom-call(bf16[256,512]{1,0:T(8,128)(2,1)S(1)} %planes.1.planes_ref, s32[128,128]{1,0:T(8,128)S(1)} %bitcast.16), custom_call_target="tpu_custom_call" | custom-call | tf_op jit(solution)/shard_map/lookup/pallas_call | solution.py:104
  93.2 2.9 %lookup.6.refs_0_ = s32[128,128]{1,0:T(8,128)S(1)} custom-call(bf16[256,512]{1,0:T(8,128)(2,1)S(1)} %planes.1.planes_ref, s32[128,128]{1,0:T(8,128)S(1)} %bitcast.17, s32[128,128]{1,0:T(8,128)S(1)} %lookup.5.refs_0_), custom_call_target="tpu_custom_call" | custom-call | tf_op jit(solution)/shard_map/lookup/pallas_call | solution.py:104
  96.1 2.3 %lookup.7.refs_0_ = s32[128,128]{1,0:T(8,128)S(1)} custom-call(bf16[256,512]{1,0:T(8,128)(2,1)S(1)} %planes.1.planes_ref, s32[128,128]{1,0:T(8,128)S(1)} %bitcast.18, s32[128,128]{1,0:T(8,128)S(1)} %lookup.6.refs_0_), custom_call_target="tpu_custom_call" | custom-call | tf_op jit(solution)/shard_map/lookup/pallas_call | solution.py:104
  102.2 1.3 stage.1
  103.5 20.2 %values.1 = (f32[128,128]{1,0:T(8,128)}, f32[32,16,128]{2,1,0:T(8,128)S(1)}, s32[32784,128]{1,0:T(8,128)S(1)}) custom-call(s32[16384]{0:T(1024)S(1)} %bitcast.23, s32[128,128]{1,0:T(8,128)S(1)} %get-tuple-element.14.odd_ref, bf16[16384,128]{1,0:T(8,128)(2,1)} %child_ref.1, s32[128,128]{1,0:T(8,128)S(1)} %bitcast.22, ...), custom_call_target="tpu_custom_call", output_to_operand_aliasing={{2}: (7, {})} | custom-call | tf_op jit(solution)/shard_map/values/pallas_call | solution.py:306
  123.7 13.1 %all_to_all.17.incoming_ref = f32[32,16,128]{2,1,0:T(8,128)S(1)} all-to-all(f32[32,16,128]{2,1,0:T(8,128)S(1)} %get-tuple-element.19), channel_id=1, replica_groups=mesh['gx'=4,'gy'=8] {'gx','gy'}, dimensions={0} | all-to-all | bytes 524288 | tf_op jit(solution)/shard_map/all_to_all | solution.py:503
  137.8 2.5 %all-to-all-start.1 = ((f32[32,1,128]{2,1,0:T(1,128)}), f32[32,1,128]{2,1,0:T(1,128)S(1)}, u32[]{:S(2)}, u32[]{:S(2)}) async-start(f32[32,1,128]{2,1,0:T(1,128)} %bitcast.10), calls=%async_computation.1 | async-start | bytes 32768 | tf_op jit(solution)/shard_map/all_to_all | solution.py:506
  140.8 6.6 %all-to-all-done.1 = f32[32,1,128]{2,1,0:T(1,128)S(1)} async-done(((f32[32,1,128]{2,1,0:T(1,128)}), f32[32,1,128]{2,1,0:T(1,128)S(1)}, u32[]{:S(2)}, u32[]{:S(2)}) %all-to-all-start.1) | async-done | bytes 16416 | tf_op jit(solution)/shard_map/all_to_all | solution.py:506
  (74 shorter events, 15.8 us)
Async XLA Ops:
  2.9 17.1 %collective-permute-start.3 = (s32[1024,128]{1,0:T(8,128)S(1)}, s32[1024,128]{1,0:T(8,128)S(1)}, u32[]{:S(2)}, u32[]{:S(2)}) collective-permute-start(s32[1024,128]{1,0:T(8,128)S(1)} %pack.1.refs_0_), channel_id=1, source_target_pairs={{0,2},{1,3},{2,4},{3,5},{4,6},{5,7},{6,0},{7,1},{8,10},{9,11},{10,... | collective-permute-start | bytes 1572872 | tf_op jit(solution)/shard_map/ppermute | solution.py:440
  6.0 14.0 %collective-permute-start.12 = (s32[1024,128]{1,0:T(8,128)S(1)}, s32[1024,128]{1,0:T(8,128)S(1)}, u32[]{:S(2)}, u32[]{:S(2)}) collective-permute-start(s32[1024,128]{1,0:T(8,128)S(1)} %pack.1.refs_0_), channel_id=1, source_target_pairs={{0,8},{1,9},{2,10},{3,11},{4,12},{5,13},{6,14},{7,15},{8,0},{9,1},... | collective-permute-start | bytes 1572872 | tf_op jit(solution)/shard_map/ppermute | solution.py:440
  6.0 15.5 %collective-permute-start.1 = (s32[1024,128]{1,0:T(8,128)S(1)}, s32[1024,128]{1,0:T(8,128)S(1)}, u32[]{:S(2)}, u32[]{:S(2)}) collective-permute-start(s32[1024,128]{1,0:T(8,128)S(1)} %pack.1.refs_0_), channel_id=1, source_target_pairs={{0,16},{1,17},{2,18},{3,19},{4,20},{5,21},{6,22},{7,23},{8,9},{9,8... | collective-permute-start | bytes 1572872 | tf_op jit(solution)/shard_map/ppermute | solution.py:440
  7.5 15.5 %collective-permute-start = (s32[1024,128]{1,0:T(8,128)S(1)}, s32[1024,128]{1,0:T(8,128)S(1)}, u32[]{:S(2)}, u32[]{:S(2)}) collective-permute-start(s32[1024,128]{1,0:T(8,128)S(1)} %pack.1.refs_0_), channel_id=1, source_target_pairs={{0,1},{1,0},{2,3},{3,2},{4,5},{5,4},{6,7},{7,6},{8,24},{9,25},{10,... | collective-permute-start | bytes 1572872 | tf_op jit(solution)/shard_map/ppermute | solution.py:440
  19.9 16.1 %collective-permute-start.7 = (s32[1024,128]{1,0:T(8,128)S(1)}, s32[1024,128]{1,0:T(8,128)S(1)}, u32[]{:S(2)}, u32[]{:S(2)}) collective-permute-start(s32[1024,128]{1,0:T(8,128)S(1)} %collective-permute-done.3.refs_4_), channel_id=1, source_target_pairs={{0,2},{1,3},{2,4},{3,5},{4,6},{5,7},{6,0},{7,1},{8,10},{9,11},{10,... | collective-permute-start | bytes 1572872 | tf_op jit(solution)/shard_map/ppermute | solution.py:440
  19.9 17.6 %collective-permute-start.5 = (s32[1024,128]{1,0:T(8,128)S(1)}, s32[1024,128]{1,0:T(8,128)S(1)}, u32[]{:S(2)}, u32[]{:S(2)}) collective-permute-start(s32[1024,128]{1,0:T(8,128)S(1)} %collective-permute-done.3.refs_4_), channel_id=1, source_target_pairs={{0,16},{1,17},{2,18},{3,19},{4,20},{5,21},{6,22},{7,23},{8,9},{9,8... | collective-permute-start | bytes 1572872 | tf_op jit(solution)/shard_map/ppermute | solution.py:440
  21.5 16.1 %collective-permute-start.4 = (s32[1024,128]{1,0:T(8,128)S(1)}, s32[1024,128]{1,0:T(8,128)S(1)}, u32[]{:S(2)}, u32[]{:S(2)}) collective-permute-start(s32[1024,128]{1,0:T(8,128)S(1)} %collective-permute-done.3.refs_4_), channel_id=1, source_target_pairs={{0,1},{1,0},{2,3},{3,2},{4,5},{5,4},{6,7},{7,6},{8,24},{9,25},{10,... | collective-permute-start | bytes 1572872 | tf_op jit(solution)/shard_map/ppermute | solution.py:440
  23.0 14.6 %collective-permute-start.14 = (s32[1024,128]{1,0:T(8,128)S(1)}, s32[1024,128]{1,0:T(8,128)S(1)}, u32[]{:S(2)}, u32[]{:S(2)}) collective-permute-start(s32[1024,128]{1,0:T(8,128)S(1)} %collective-permute-done.1.refs_2_), channel_id=1, source_target_pairs={{0,8},{1,9},{2,10},{3,11},{4,12},{5,13},{6,14},{7,15},{8,0},{9,1},... | collective-permute-start | bytes 1572872 | tf_op jit(solution)/shard_map/ppermute | solution.py:440
  23.0 15.5 %collective-permute-start.13 = (s32[1024,128]{1,0:T(8,128)S(1)}, s32[1024,128]{1,0:T(8,128)S(1)}, u32[]{:S(2)}, u32[]{:S(2)}) collective-permute-start(s32[1024,128]{1,0:T(8,128)S(1)} %collective-permute-done.refs_1_), channel_id=1, source_target_pairs={{0,8},{1,9},{2,10},{3,11},{4,12},{5,13},{6,14},{7,15},{8,0},{9,1},... | collective-permute-start | bytes 1572872 | tf_op jit(solution)/shard_map/ppermute | solution.py:440
  37.6 16.1 %collective-permute-start.10 = (s32[1024,128]{1,0:T(8,128)S(1)}, s32[1024,128]{1,0:T(8,128)S(1)}, u32[]{:S(2)}, u32[]{:S(2)}) collective-permute-start(s32[1024,128]{1,0:T(8,128)S(1)} %collective-permute-done.7.refs_8_), channel_id=1, source_target_pairs={{0,2},{1,3},{2,4},{3,5},{4,6},{5,7},{6,0},{7,1},{8,10},{9,11},{10,... | collective-permute-start | bytes 1572872 | tf_op jit(solution)/shard_map/ppermute | solution.py:440
  37.7 18.8 %collective-permute-start.9 = (s32[1024,128]{1,0:T(8,128)S(1)}, s32[1024,128]{1,0:T(8,128)S(1)}, u32[]{:S(2)}, u32[]{:S(2)}) collective-permute-start(s32[1024,128]{1,0:T(8,128)S(1)} %collective-permute-done.7.refs_8_), channel_id=1, source_target_pairs={{0,16},{1,17},{2,18},{3,19},{4,20},{5,21},{6,22},{7,23},{8,9},{9,8... | collective-permute-start | bytes 1572872 | tf_op jit(solution)/shard_map/ppermute | solution.py:440
  38.5 18.0 %collective-permute-start.8 = (s32[1024,128]{1,0:T(8,128)S(1)}, s32[1024,128]{1,0:T(8,128)S(1)}, u32[]{:S(2)}, u32[]{:S(2)}) collective-permute-start(s32[1024,128]{1,0:T(8,128)S(1)} %collective-permute-done.7.refs_8_), channel_id=1, source_target_pairs={{0,1},{1,0},{2,3},{3,2},{4,5},{5,4},{6,7},{7,6},{8,24},{9,25},{10,... | collective-permute-start | bytes 1572872 | tf_op jit(solution)/shard_map/ppermute | solution.py:440
  56.5 14.4 %collective-permute-start.6 = (s32[1024,128]{1,0:T(8,128)S(1)}, s32[1024,128]{1,0:T(8,128)S(1)}, u32[]{:S(2)}, u32[]{:S(2)}) collective-permute-start(s32[1024,128]{1,0:T(8,128)S(1)} %collective-permute-done.2.refs_3_), channel_id=1, source_target_pairs={{0,2},{1,3},{2,4},{3,5},{4,6},{5,7},{6,0},{7,1},{8,10},{9,11},{10,... | collective-permute-start | bytes 1572872 | tf_op jit(solution)/shard_map/ppermute | solution.py:440
  56.5 14.4 %collective-permute-start.24 = (s32[1024,128]{1,0:T(8,128)S(1)}, s32[1024,128]{1,0:T(8,128)S(1)}, u32[]{:S(2)}, u32[]{:S(2)}) collective-permute-start(s32[1024,128]{1,0:T(8,128)S(1)} %collective-permute-done.10.refs_11_), channel_id=1, source_target_pairs={{0,16},{1,17},{2,18},{3,19},{4,20},{5,21},{6,22},{7,23},{8,9},{9,8... | collective-permute-start | bytes 1572872 | tf_op jit(solution)/shard_map/ppermute | solution.py:440
  58.0 12.9 %collective-permute-start.11 = (s32[1024,128]{1,0:T(8,128)S(1)}, s32[1024,128]{1,0:T(8,128)S(1)}, u32[]{:S(2)}, u32[]{:S(2)}) collective-permute-start(s32[1024,128]{1,0:T(8,128)S(1)} %collective-permute-done.10.refs_11_), channel_id=1, source_target_pairs={{0,1},{1,0},{2,3},{3,2},{4,5},{5,4},{6,7},{7,6},{8,24},{9,25},{10,... | collective-permute-start | bytes 1572872 | tf_op jit(solution)/shard_map/ppermute | solution.py:440
  59.5 13.0 %collective-permute-start.22 = (s32[1024,128]{1,0:T(8,128)S(1)}, s32[1024,128]{1,0:T(8,128)S(1)}, u32[]{:S(2)}, u32[]{:S(2)}) collective-permute-start(s32[1024,128]{1,0:T(8,128)S(1)} %collective-permute-done.10.refs_11_), channel_id=1, source_target_pairs={{0,8},{1,9},{2,10},{3,11},{4,12},{5,13},{6,14},{7,15},{8,0},{9,1},... | collective-permute-start | bytes 1572872 | tf_op jit(solution)/shard_map/ppermute | solution.py:440
  59.5 13.2 %collective-permute-start.21 = (s32[1024,128]{1,0:T(8,128)S(1)}, s32[1024,128]{1,0:T(8,128)S(1)}, u32[]{:S(2)}, u32[]{:S(2)}) collective-permute-start(s32[1024,128]{1,0:T(8,128)S(1)} %collective-permute-done.9.refs_10_), channel_id=1, source_target_pairs={{0,8},{1,9},{2,10},{3,11},{4,12},{5,13},{6,14},{7,15},{8,0},{9,1},... | collective-permute-start | bytes 1572872 | tf_op jit(solution)/shard_map/ppermute | solution.py:440
  70.9 16.1 %collective-permute-start.23 = (s32[1024,128]{1,0:T(8,128)S(1)}, s32[1024,128]{1,0:T(8,128)S(1)}, u32[]{:S(2)}, u32[]{:S(2)}) collective-permute-start(s32[1024,128]{1,0:T(8,128)S(1)} %collective-permute-done.6.refs_7_), channel_id=1, source_target_pairs={{0,2},{1,3},{2,4},{3,5},{4,6},{5,7},{6,0},{7,1},{8,10},{9,11},{10,... | collective-permute-start | bytes 1572872 | tf_op jit(solution)/shard_map/ppermute | solution.py:440
  70.9 16.1 %collective-permute-start.25 = (s32[1024,128]{1,0:T(8,128)S(1)}, s32[1024,128]{1,0:T(8,128)S(1)}, u32[]{:S(2)}, u32[]{:S(2)}) collective-permute-start(s32[1024,128]{1,0:T(8,128)S(1)} %collective-permute-done.11.refs_12_), channel_id=1, source_target_pairs={{0,16},{1,17},{2,18},{3,19},{4,20},{5,21},{6,22},{7,23},{8,9},{9,8... | collective-permute-start | bytes 1572872 | tf_op jit(solution)/shard_map/ppermute | solution.py:440
  72.5 30.9 %collective-permute-start.26 = (s32[1024,128]{1,0:T(8,128)S(1)}, s32[1024,128]{1,0:T(8,128)S(1)}, u32[]{:S(2)}, u32[]{:S(2)}) collective-permute-start(s32[1024,128]{1,0:T(8,128)S(1)} %collective-permute-done.6.refs_7_), channel_id=1, source_target_pairs={{0,8},{1,9},{2,10},{3,11},{4,12},{5,13},{6,14},{7,15},{8,0},{9,1},... | collective-permute-start | bytes 1572872 | tf_op jit(solution)/shard_map/ppermute | solution.py:440
  72.7 30.7 %collective-permute-start.28 = (s32[1024,128]{1,0:T(8,128)S(1)}, s32[1024,128]{1,0:T(8,128)S(1)}, u32[]{:S(2)}, u32[]{:S(2)}) collective-permute-start(s32[1024,128]{1,0:T(8,128)S(1)} %collective-permute-done.11.refs_12_), channel_id=1, source_target_pairs={{0,8},{1,9},{2,10},{3,11},{4,12},{5,13},{6,14},{7,15},{8,0},{9,1},... | collective-permute-start | bytes 1572872 | tf_op jit(solution)/shard_map/ppermute | solution.py:440
  73.0 30.4 %collective-permute-start.29 = (s32[1024,128]{1,0:T(8,128)S(1)}, s32[1024,128]{1,0:T(8,128)S(1)}, u32[]{:S(2)}, u32[]{:S(2)}) collective-permute-start(s32[1024,128]{1,0:T(8,128)S(1)} %collective-permute-done.24.rest_6_), channel_id=1, source_target_pairs={{0,8},{1,9},{2,10},{3,11},{4,12},{5,13},{6,14},{7,15},{8,0},{9,1},... | collective-permute-start | bytes 1572872 | tf_op jit(solution)/shard_map/ppermute | solution.py:440
  87.0 16.4 %collective-permute-start.27 = (s32[1024,128]{1,0:T(8,128)S(1)}, s32[1024,128]{1,0:T(8,128)S(1)}, u32[]{:S(2)}, u32[]{:S(2)}) collective-permute-start(s32[1024,128]{1,0:T(8,128)S(1)} %collective-permute-done.23.rest_5_), channel_id=1, source_target_pairs={{0,8},{1,9},{2,10},{3,11},{4,12},{5,13},{6,14},{7,15},{8,0},{9,1},... | collective-permute-start | bytes 1572872 | tf_op jit(solution)/shard_map/ppermute | solution.py:440
  87.0 16.4 %collective-permute-start.30 = (s32[1024,128]{1,0:T(8,128)S(1)}, s32[1024,128]{1,0:T(8,128)S(1)}, u32[]{:S(2)}, u32[]{:S(2)}) collective-permute-start(s32[1024,128]{1,0:T(8,128)S(1)} %collective-permute-done.25.rest_7_), channel_id=1, source_target_pairs={{0,8},{1,9},{2,10},{3,11},{4,12},{5,13},{6,14},{7,15},{8,0},{9,1},... | collective-permute-start | bytes 1572872 | tf_op jit(solution)/shard_map/ppermute | solution.py:440
  (18 other events, 308.3 us)

commit v2 on v1

--- a/solution.py
+++ b/solution.py
@@ -12,7 +12,7 @@
 LANES = 128
 SCALE_BITS = 17
 TABLE_LIMIT = 24 * 2**20
-CHUNKS = 8
+UNIT, WIDEST = float(2**20), 32767.0
 SHARES = (5, 5, 4, 1, 1)
 STAGED = tuple(i for i in range(16) if i not in (11, 14, 15))
 STAGED += tuple(16 + i for i in range(16) if i not in (7, 11, 13, 14, 15))
@@ -148,7 +148,7 @@
 
 def outgoing(value_ref, row_ref, reach_ref, slot_ref, note_ref, out_ref, weighted):
     table = jnp.concatenate(split(value_ref[...].T, 2), axis=1)
-    group = 8
+    group = 16
 
     def step(i, carry):
         queries = [row_ref[pl.ds(group * i + k, 1), :] for k in range(group)]
@@ -158,21 +158,30 @@
         return carry
 
     lax.fori_loop(0, row_ref.shape[0] // group, step, 0)
-    devices, tall = note_ref.shape[0], out_ref.shape[1]
-    limit = tall // 2
+    devices, limit = note_ref.shape[0], out_ref.shape[1]
+    half = limit // 2
     place = one_hot(iota((devices * limit, row_ref.shape[0]), 0) == slot_ref[...])
     total = jnp.zeros((devices * limit, LANES), jnp.float32)
     for part in split(weighted[...] * column(reach_ref[...]), 3):
         total = total + jnp.dot(place, part, preferred_element_type=jnp.float32)
+    top = jnp.max(jnp.abs(total), axis=1, keepdims=True)
+    scale = jnp.floor(top * UNIT) + 1.0
+    coded = jnp.floor(total * (WIDEST * UNIT / scale) + 0.5).astype(jnp.int32)
+    lane = iota((limit, LANES), 1)
+    spot = iota((limit, LANES), 0) + (limit + 1)
     for d in range(devices):
-        out_ref[d, :limit, :] = total[limit * d : limit * (d + 1)]
-        out_ref[d, limit:, :] = jnp.broadcast_to(note_ref[d : d + 1, :], (limit, LANES))
+        rows = slice(limit * d, limit * (d + 1))
+        scales = jnp.where(lane == spot, jnp.broadcast_to(scale[rows], lane.shape), 0.0)
+        note = note_ref[d : d + 1, :] + jnp.sum(scales, axis=0, keepdims=True)
+        low, high = coded[rows][:half], coded[rows][half:]
+        out_ref[d, :half, :] = (low & 0xFFFF) | (high << 16)
+        out_ref[d, half:, :] = jnp.broadcast_to(note.astype(jnp.int32), (limit - half, LANES))
 
 
 def outgoing_rows(history_value, child_row, reach, slot, notes, limit):
     return pl.pallas_call(
         outgoing,
-        out_shape=jax.ShapeDtypeStruct((notes.shape[0], 2 * limit, LANES), jnp.float32),
+        out_shape=jax.ShapeDtypeStruct((notes.shape[0], limit, LANES), jnp.int32),
         scratch_shapes=[pltpu.VMEM(child_row.shape, jnp.float32)],
         compiler_params=room(4 * 2**20),
         name="outgoing",
@@ -196,9 +205,10 @@
     return whole, x - whole * n
 
 
-def stage_body(slots, along, width, words, home_ref, *refs):
-    block_refs, (table, place_ref, odd_ref, sems) = refs[: len(slots)], refs[len(slots) :]
+def stage_body(slots, along, width, words, home_ref, child_ref, *refs):
+    block_refs, (table, place_ref, odd_ref, child, sems) = refs[: len(slots)], refs[len(slots) :]
     copies = fill(block_refs, slots, table, sems)
+    copies.append(pltpu.make_async_copy(child_ref, child, sems.at[len(slots)]))
     for copy in copies:
         copy.start()
     depth = along // width
@@ -222,7 +232,7 @@
         copy.wait()
 
 
-def staged(blocks, home, along, width):
+def staged(blocks, home, child_value, along, width):
     size = blocks[0].shape[0]
     vmem, _, hbm = spaces()
     shape = (len(blocks) * size + 16, LANES)
@@ -232,30 +242,27 @@
             jax.ShapeDtypeStruct(shape, jnp.int32),
             jax.ShapeDtypeStruct(home.shape[::-1], jnp.int32),
             jax.ShapeDtypeStruct(home.shape, jnp.int32),
+            jax.ShapeDtypeStruct(child_value.shape, child_value.dtype),
         ),
-        in_specs=[vmem] + [hbm] * len(STAGED),
-        out_specs=(vmem, vmem, vmem),
-        scratch_shapes=[pltpu.SemaphoreType.DMA((len(STAGED),))],
+        in_specs=[vmem, pl.BlockSpec(memory_space=pltpu.HBM)] + [hbm] * len(STAGED),
+        out_specs=(vmem, vmem, vmem, vmem),
+        scratch_shapes=[pltpu.SemaphoreType.DMA((len(STAGED) + 1,))],
         compiler_params=room(0),
         name="stage",
-    )(home, *(blocks[b] for b in STAGED))
-
-
-def value_body(slots, place_ref, odd_ref, child_ref, *rest):
+    )(
+        home,
+        pltpu.with_memory_space_constraint(child_value, pltpu.HBM),
+        *(blocks[b] for b in STAGED),
+    )
+
+
+def value_body(slots, place_ref, odd_ref, child, *rest):
     upper, block_refs = rest[:4], rest[5 : 5 + len(slots)]
-    value_ref, out_ref, table, child, weighted, sems, arrived = rest[5 + len(slots) :]
+    value_ref, out_ref, table, weighted, sems = rest[5 + len(slots) :]
     copies = fill(block_refs, slots, table, sems)
     tiles = value_ref.shape[0]
-    chunk = tiles // CHUNKS
-
-    def children_of(c):
-        rows = pl.ds(c * chunk * LANES, chunk * LANES)
-        return pltpu.make_async_copy(child_ref.at[rows, :], child.at[rows, :], arrived.at[c])
-
     for copy in copies:
         copy.start()
-    for c in range(CHUNKS):
-        children_of(c).start()
     for copy in copies:
         copy.wait()
     sub = iota((8, LANES), 0)
@@ -289,44 +296,34 @@
         value_ref[pl.ds(t, 1), :] = picked * (0.5**SCALE_BITS)
         return carry
 
-    def stretch(c, carry):
-        children_of(c).wait()
-        return lax.fori_loop(
-            0, chunk, lambda i, carry: tile(c * chunk + i, carry), carry, unroll=4
-        )
-
-    lax.fori_loop(0, CHUNKS, stretch, 0)
+    lax.fori_loop(0, tiles, tile, 0, unroll=16)
     outgoing(value_ref, *upper, out_ref, weighted)
 
 
 def values_from(blocks, home, along, width, child_value, child_row, reach, slot, notes, limit):
-    table, place, odd = staged(blocks, home, along, width)
+    table, place, odd, child = staged(blocks, home, child_value, along, width)
     rest = tuple(b for b in range(len(blocks)) if b not in STAGED)
     vmem, smem, hbm = spaces()
     return pl.pallas_call(
         functools.partial(value_body, rest),
         out_shape=(
             jax.ShapeDtypeStruct(odd.shape, jnp.float32),
-            jax.ShapeDtypeStruct((notes.shape[0], 2 * limit, LANES), jnp.float32),
+            jax.ShapeDtypeStruct((notes.shape[0], limit, LANES), jnp.int32),
             jax.ShapeDtypeStruct(table.shape, table.dtype),
         ),
-        in_specs=[smem, vmem, pl.BlockSpec(memory_space=pltpu.HBM)]
-        + [vmem] * 5
-        + [hbm] * len(rest),
+        in_specs=[smem] + [vmem] * 7 + [hbm] * len(rest),
         out_specs=(vmem, vmem, vmem),
         scratch_shapes=[
-            pltpu.VMEM(child_value.shape, child_value.dtype),
             pltpu.VMEM(child_row.shape, jnp.float32),
             pltpu.SemaphoreType.DMA((len(rest),)),
-            pltpu.SemaphoreType.DMA((CHUNKS,)),
         ],
         input_output_aliases={7: 2},
-        compiler_params=room(8 * 2**20),
+        compiler_params=room(4 * 2**20),
         name="values",
     )(
         place.reshape(-1),
         odd,
-        pltpu.with_memory_space_constraint(child_value, pltpu.HBM),
+        child,
         child_row,
         reach,
         slot,
@@ -362,7 +359,9 @@
     ranks = one_hot(column(rank) == iota((parents, LANES), 1).astype(jnp.float32))
     asked = jnp.dot(rows, ranks, preferred_element_type=jnp.float32) - 1.0
     reach = jnp.sum(jnp.broadcast_to(reach_ref[...], note_ref.shape), axis=1, keepdims=True)
-    note_ref[...] = jnp.where(iota(note_ref.shape, 1) == limit, reach, asked)
+    lane = iota(note_ref.shape, 1)
+    note = jnp.where(lane == limit, jnp.floor(reach * UNIT + 0.5), asked)
+    note_ref[...] = jnp.where(lane > limit, 0.0, note)
 
 
 def slots_of(br_home, br_set, reach, per_br, devices, limit):
@@ -379,18 +378,21 @@
 
 def regret_body(incoming_ref, cum_ref, gap_ref, total_ref, reach_ref):
     sets = cum_ref.shape[0]
-    devices, limit = incoming_ref.shape[0], incoming_ref.shape[1] // 2
-    notes = jnp.concatenate([incoming_ref[d, limit : limit + 1, :] for d in range(devices)], axis=0)
-    lane = iota((devices, LANES), 1)
+    devices, limit = incoming_ref.shape[:2]
+    half = limit // 2
+    coded, spread, notes = [], [], []
+    for d in range(devices):
+        pair = incoming_ref[d, :half, :]
+        coded += [(pair << 16) >> 16, pair >> 16]
+        notes.append(incoming_ref[d, half : half + 1, :].astype(jnp.float32))
+        spread.append(jnp.broadcast_to(notes[-1], (limit, LANES)))
+    spread, notes = jnp.concatenate(spread, axis=0), jnp.concatenate(notes, axis=0)
+    lane, turn = iota(spread.shape, 1), iota(spread.shape, 0) % limit
+    asked = jnp.sum(jnp.where(lane == turn, spread, 0.0), axis=1, keepdims=True)
+    scale = jnp.sum(jnp.where(lane == turn + (limit + 1), spread, 0.0), axis=1, keepdims=True)
+    rows = jnp.concatenate(coded, axis=0).astype(jnp.float32) * (scale * (1.0 / (WIDEST * UNIT)))
+    member = one_hot(jnp.broadcast_to(asked, spread.shape) == lane.astype(jnp.float32))
     value = jnp.zeros(cum_ref.shape, jnp.float32)
-    rows = jnp.concatenate([incoming_ref[d, :limit, :] for d in range(devices)], axis=0)
-    spread = jnp.concatenate(
-        [jnp.broadcast_to(notes[d : d + 1, :], (limit, LANES)) for d in range(devices)], axis=0
-    )
-    mine = iota(spread.shape, 1) == iota(spread.shape, 0) % limit
-    asked = jnp.sum(jnp.where(mine, spread, 0.0), axis=1, keepdims=True)
-    wide = jnp.broadcast_to(asked, spread.shape)
-    member = one_hot(wide == iota(spread.shape, 1).astype(jnp.float32))
     for part in split(rows, 3):
         value = value + lax.dot_general(
             member, part, (((0,), (0,)), ((), ())), preferred_element_type=jnp.float32
@@ -401,9 +403,10 @@
     gap_ref[...] = jnp.sum(jnp.where(own, gap, 0.0), axis=0, keepdims=True)
     total = jnp.sum(jnp.broadcast_to(gap, (sets, LANES)), axis=0, keepdims=True)
     total_ref[...] = jnp.broadcast_to(total, total_ref.shape)
-    reach = jnp.sum(jnp.where(lane == limit, notes, 0.0), axis=1, keepdims=True)
+    here = iota(notes.shape, 1) == limit
+    reach = jnp.sum(jnp.where(here, notes, 0.0), axis=1, keepdims=True)
     reach = jnp.sum(jnp.broadcast_to(reach, notes.shape), axis=0, keepdims=True)
-    reach_ref[...] = reach
+    reach_ref[...] = reach * (1.0 / UNIT)
 
 
 def regrets(incoming, br_cum):

time: 150 us -> 145 us (0.967)
  blocking collectives: 13.1 us -> 10.4 us
  Pallas kernels: 33.4 us -> 30.8 us
    pallas_call x1, Pallas kernels: 20.2 us -> 15.5 us  [values_from(): pl.pallas_call(functools.partial(value_body, rest), out_shape=(jax.ShapeD...]
    all_to_all x1, blocking collectives: 13.1 us -> 10.4 us  [local(): lax.all_to_all(outgoing_two, AXES, split_axis=0, concat_axis=0, tiled=True)]
    pallas_call x1, Pallas kernels: 1.27 us -> 3.34 us  [staged(): pl.pallas_call(functools.partial(stage_body, STAGED, along, width, size),...]
  transfers between devices with their start and end apart: 32 -> 32, of which waited for: 8 -> 8; matrix products, arithmetic and copies ran while one was open for 0% -> 0% of each run, Pallas kernels for 7% -> 9%
where the time goes in v2:
time: 145 us
  waiting for transfers between devices  71.1 us (49%)
  Pallas kernels  30.8 us (21%)
  starting transfers between devices  22.7 us (16%)
  blocking collectives  10.4 us (7%)
  local copies, waits for them, and re-layouts  6.37 us (4%)
  between operations  2.7 us (2%)
    ppermute x31, waiting for transfers between devices, move(): return lax.ppermute(array, AXES, pairs)  64.4 us
    ppermute x31, starting transfers between devices, move(): return lax.ppermute(array, AXES, pairs)  20.2 us
    pallas_call x1, Pallas kernels, values_from(): pl.pallas_call(functools.partial(value_body, rest), out_shape=(jax.ShapeD...  15.5 us
    all_to_all x1, blocking collectives, local(): lax.all_to_all(outgoing_two, AXES, split_axis=0, concat_axis=0, tiled=True)  10.4 us
    pallas_call x5, Pallas kernels, lookups(): pl.pallas_call(functools.partial(lookup_body, first, last), out_shape=jax...  9.2 us
    all_to_all x1, waiting for transfers between devices, local(): gaps = lax.all_to_all(gaps, AXES, split_axis=0, concat_axis=0, tiled=True)  6.63 us
    unnamed x20, local copies, waits for them, and re-layouts  5.85 us
    pallas_call x1, Pallas kernels, staged(): pl.pallas_call(functools.partial(stage_body, STAGED, along, width, size),...  3.34 us
  transfers between devices with their start and end apart: 32, of which 8 were waited for; matrix products, arithmetic and copies ran while one was open for 0% of the time, Pallas kernels for 9%

profile of v2, /device:TPU:0, one launch (start us, length us, event | category | flops | bytes accessed | tf_op | source)
XLA Modules:
  0.0 144.6 jit_solution(12942671065182300350)
XLA Ops:
  2.9 3.1 %collective-permute-start.3 = (s32[1024,128]{1,0:T(8,128)S(1)}, s32[1024,128]{1,0:T(8,128)S(1)}, u32[]{:S(2)}, u32[]{:S(2)}) collective-permute-start(s32[1024,128]{1,0:T(8,128)S(1)} %pack.1.refs_0_), channel_id=1, source_target_pairs={{0,2},{1,3},{2,4},{3,5},{4,6},{5,7},{6,0},{7,1},{8,10},{9,11},{10,... | collective-permute-start | bytes 1572872 | tf_op jit(solution)/shard_map/ppermute | solution.py:443
  6.0 1.5 %collective-permute-start.1 = (s32[1024,128]{1,0:T(8,128)S(1)}, s32[1024,128]{1,0:T(8,128)S(1)}, u32[]{:S(2)}, u32[]{:S(2)}) collective-permute-start(s32[1024,128]{1,0:T(8,128)S(1)} %pack.1.refs_0_), channel_id=1, source_target_pairs={{0,16},{1,17},{2,18},{3,19},{4,20},{5,21},{6,22},{7,23},{8,9},{9,8... | collective-permute-start | bytes 1572872 | tf_op jit(solution)/shard_map/ppermute | solution.py:443
  7.5 1.5 %collective-permute-start = (s32[1024,128]{1,0:T(8,128)S(1)}, s32[1024,128]{1,0:T(8,128)S(1)}, u32[]{:S(2)}, u32[]{:S(2)}) collective-permute-start(s32[1024,128]{1,0:T(8,128)S(1)} %pack.1.refs_0_), channel_id=1, source_target_pairs={{0,1},{1,0},{2,3},{3,2},{4,5},{5,4},{6,7},{7,6},{8,24},{9,25},{10,... | collective-permute-start | bytes 1572872 | tf_op jit(solution)/shard_map/ppermute | solution.py:443
  9.0 10.9 %collective-permute-done.3.refs_4_ = s32[1024,128]{1,0:T(8,128)S(1)} collective-permute-done((s32[1024,128]{1,0:T(8,128)S(1)}, s32[1024,128]{1,0:T(8,128)S(1)}, u32[]{:S(2)}, u32[]{:S(2)}) %collective-permute-start.3) | collective-permute-done | bytes 524320 | tf_op jit(solution)/shard_map/ppermute | solution.py:443
  19.9 1.6 %collective-permute-start.5 = (s32[1024,128]{1,0:T(8,128)S(1)}, s32[1024,128]{1,0:T(8,128)S(1)}, u32[]{:S(2)}, u32[]{:S(2)}) collective-permute-start(s32[1024,128]{1,0:T(8,128)S(1)} %collective-permute-done.3.refs_4_), channel_id=1, source_target_pairs={{0,16},{1,17},{2,18},{3,19},{4,20},{5,21},{6,22},{7,23},{8,9},{9,8... | collective-permute-start | bytes 1572872 | tf_op jit(solution)/shard_map/ppermute | solution.py:443
  21.5 1.5 %collective-permute-start.4 = (s32[1024,128]{1,0:T(8,128)S(1)}, s32[1024,128]{1,0:T(8,128)S(1)}, u32[]{:S(2)}, u32[]{:S(2)}) collective-permute-start(s32[1024,128]{1,0:T(8,128)S(1)} %collective-permute-done.3.refs_4_), channel_id=1, source_target_pairs={{0,1},{1,0},{2,3},{3,2},{4,5},{5,4},{6,7},{7,6},{8,24},{9,25},{10,... | collective-permute-start | bytes 1572872 | tf_op jit(solution)/shard_map/ppermute | solution.py:443
  23.5 12.5 %collective-permute-done.7.refs_8_ = s32[1024,128]{1,0:T(8,128)S(1)} collective-permute-done((s32[1024,128]{1,0:T(8,128)S(1)}, s32[1024,128]{1,0:T(8,128)S(1)}, u32[]{:S(2)}, u32[]{:S(2)}) %collective-permute-start.7) | collective-permute-done | bytes 524320 | tf_op jit(solution)/shard_map/ppermute | solution.py:443
  36.1 1.5 %collective-permute-start.2 = (s32[1024,128]{1,0:T(8,128)S(1)}, s32[1024,128]{1,0:T(8,128)S(1)}, u32[]{:S(2)}, u32[]{:S(2)}) collective-permute-start(s32[1024,128]{1,0:T(8,128)S(1)} %collective-permute-done.refs_1_), channel_id=1, source_target_pairs={{0,16},{1,17},{2,18},{3,19},{4,20},{5,21},{6,22},{7,23},{8,9},{9,8... | collective-permute-start | bytes 1572872 | tf_op jit(solution)/shard_map/ppermute | solution.py:443
  39.7 8.8 %collective-permute-done.2.refs_3_ = s32[1024,128]{1,0:T(8,128)S(1)} collective-permute-done((s32[1024,128]{1,0:T(8,128)S(1)}, s32[1024,128]{1,0:T(8,128)S(1)}, u32[]{:S(2)}, u32[]{:S(2)}) %collective-permute-start.2) | collective-permute-done | bytes 524320 | tf_op jit(solution)/shard_map/ppermute | solution.py:443
  49.1 4.7 %collective-permute-done.10.refs_11_ = s32[1024,128]{1,0:T(8,128)S(1)} collective-permute-done((s32[1024,128]{1,0:T(8,128)S(1)}, s32[1024,128]{1,0:T(8,128)S(1)}, u32[]{:S(2)}, u32[]{:S(2)}) %collective-permute-start.10) | collective-permute-done | bytes 524320 | tf_op jit(solution)/shard_map/ppermute | solution.py:443
  53.7 2.7 %collective-permute-done.9.refs_10_ = s32[1024,128]{1,0:T(8,128)S(1)} collective-permute-done((s32[1024,128]{1,0:T(8,128)S(1)}, s32[1024,128]{1,0:T(8,128)S(1)}, u32[]{:S(2)}, u32[]{:S(2)}) %collective-permute-start.9) | collective-permute-done | bytes 524320 | tf_op jit(solution)/shard_map/ppermute | solution.py:443
  56.5 1.5 %collective-permute-start.24 = (s32[1024,128]{1,0:T(8,128)S(1)}, s32[1024,128]{1,0:T(8,128)S(1)}, u32[]{:S(2)}, u32[]{:S(2)}) collective-permute-start(s32[1024,128]{1,0:T(8,128)S(1)} %collective-permute-done.10.refs_11_), channel_id=1, source_target_pairs={{0,16},{1,17},{2,18},{3,19},{4,20},{5,21},{6,22},{7,23},{8,9},{9,8... | collective-permute-start | bytes 1572872 | tf_op jit(solution)/shard_map/ppermute | solution.py:443
  58.0 1.5 %collective-permute-start.11 = (s32[1024,128]{1,0:T(8,128)S(1)}, s32[1024,128]{1,0:T(8,128)S(1)}, u32[]{:S(2)}, u32[]{:S(2)}) collective-permute-start(s32[1024,128]{1,0:T(8,128)S(1)} %collective-permute-done.10.refs_11_), channel_id=1, source_target_pairs={{0,1},{1,0},{2,3},{3,2},{4,5},{5,4},{6,7},{7,6},{8,24},{9,25},{10,... | collective-permute-start | bytes 1572872 | tf_op jit(solution)/shard_map/ppermute | solution.py:443
  60.0 10.9 %collective-permute-done.6.refs_7_ = s32[1024,128]{1,0:T(8,128)S(1)} collective-permute-done((s32[1024,128]{1,0:T(8,128)S(1)}, s32[1024,128]{1,0:T(8,128)S(1)}, u32[]{:S(2)}, u32[]{:S(2)}) %collective-permute-start.6) | collective-permute-done | bytes 524320 | tf_op jit(solution)/shard_map/ppermute | solution.py:443
  70.9 1.6 %collective-permute-start.25 = (s32[1024,128]{1,0:T(8,128)S(1)}, s32[1024,128]{1,0:T(8,128)S(1)}, u32[]{:S(2)}, u32[]{:S(2)}) collective-permute-start(s32[1024,128]{1,0:T(8,128)S(1)} %collective-permute-done.11.refs_12_), channel_id=1, source_target_pairs={{0,16},{1,17},{2,18},{3,19},{4,20},{5,21},{6,22},{7,23},{8,9},{9,8... | collective-permute-start | bytes 1572872 | tf_op jit(solution)/shard_map/ppermute | solution.py:443
  73.2 13.8 %collective-permute-done.23.rest_5_ = s32[1024,128]{1,0:T(8,128)S(1)} collective-permute-done((s32[1024,128]{1,0:T(8,128)S(1)}, s32[1024,128]{1,0:T(8,128)S(1)}, u32[]{:S(2)}, u32[]{:S(2)}) %collective-permute-start.23) | collective-permute-done | bytes 524320 | tf_op jit(solution)/shard_map/ppermute | solution.py:443
  89.5 2.9 %lookup.5.refs_0_ = s32[128,128]{1,0:T(8,128)S(1)} custom-call(bf16[256,512]{1,0:T(8,128)(2,1)S(1)} %planes.1.planes_ref, s32[128,128]{1,0:T(8,128)S(1)} %bitcast.16), custom_call_target="tpu_custom_call" | custom-call | tf_op jit(solution)/shard_map/lookup/pallas_call | solution.py:104
  93.2 2.9 %lookup.6.refs_0_ = s32[128,128]{1,0:T(8,128)S(1)} custom-call(bf16[256,512]{1,0:T(8,128)(2,1)S(1)} %planes.1.planes_ref, s32[128,128]{1,0:T(8,128)S(1)} %bitcast.17, s32[128,128]{1,0:T(8,128)S(1)} %lookup.5.refs_0_), custom_call_target="tpu_custom_call" | custom-call | tf_op jit(solution)/shard_map/lookup/pallas_call | solution.py:104
  96.1 2.3 %lookup.7.refs_0_ = s32[128,128]{1,0:T(8,128)S(1)} custom-call(bf16[256,512]{1,0:T(8,128)(2,1)S(1)} %planes.1.planes_ref, s32[128,128]{1,0:T(8,128)S(1)} %bitcast.18, s32[128,128]{1,0:T(8,128)S(1)} %lookup.6.refs_0_), custom_call_target="tpu_custom_call" | custom-call | tf_op jit(solution)/shard_map/lookup/pallas_call | solution.py:104
  102.2 3.3 %stage.1 = (s32[32784,128]{1,0:T(8,128)S(1)}, s32[128,128]{1,0:T(8,128)S(1)}, s32[128,128]{1,0:T(8,128)S(1)}, bf16[16384,128]{1,0:T(8,128)(2,1)S(1)}) custom-call(s32[128,128]{1,0:T(8,128)S(1)} %lookup.9.home_ref, bf16[16384,128]{1,0:T(8,128)(2,1)} %child_ref.1, s32[1024,128]{1,0:T(8,128)S(1)} %pack.1.refs_0_, s32[1024,128]{1,0:T(8,128)S(1)} %collective-permute-done.refs_1_, ...), custom_call_target="tpu_custom_call" | custom-call | tf_op jit(solution)/shard_map/stage/pallas_call | solution.py:239
  105.6 15.5 %values.1 = (f32[128,128]{1,0:T(8,128)}, s32[32,8,128]{2,1,0:T(8,128)S(1)}, s32[32784,128]{1,0:T(8,128)S(1)}) custom-call(s32[16384]{0:T(1024)S(1)} %bitcast.23, s32[128,128]{1,0:T(8,128)S(1)} %get-tuple-element.15.odd_ref, bf16[16384,128]{1,0:T(8,128)(2,1)S(1)} %get-tuple-element.16.child, ...), custom_call_target="tpu_custom_call", output_to_operand_aliasing={{2}: (7, {})} | custom-call | tf_op jit(solution)/shard_map/values/pallas_call | solution.py:307
  121.1 10.4 %all_to_all.17.incoming_ref = s32[32,8,128]{2,1,0:T(8,128)S(1)} all-to-all(s32[32,8,128]{2,1,0:T(8,128)S(1)} %get-tuple-element.21), channel_id=1, replica_groups=mesh['gx'=4,'gy'=8] {'gx','gy'}, dimensions={0} | all-to-all | bytes 262144 | tf_op jit(solution)/shard_map/all_to_all | solution.py:506
  132.6 2.5 %all-to-all-start.1 = ((f32[32,1,128]{2,1,0:T(1,128)}), f32[32,1,128]{2,1,0:T(1,128)S(1)}, u32[]{:S(2)}, u32[]{:S(2)}) async-start(f32[32,1,128]{2,1,0:T(1,128)} %bitcast.10), calls=%async_computation.1 | async-start | bytes 32768 | tf_op jit(solution)/shard_map/all_to_all | solution.py:509
  135.6 6.6 %all-to-all-done.1 = f32[32,1,128]{2,1,0:T(1,128)S(1)} async-done(((f32[32,1,128]{2,1,0:T(1,128)}), f32[32,1,128]{2,1,0:T(1,128)S(1)}, u32[]{:S(2)}, u32[]{:S(2)}) %all-to-all-start.1) | async-done | bytes 16416 | tf_op jit(solution)/shard_map/all_to_all | solution.py:509
  (74 shorter events, 15.8 us)
Async XLA Ops:
  2.9 17.1 %collective-permute-start.3 = (s32[1024,128]{1,0:T(8,128)S(1)}, s32[1024,128]{1,0:T(8,128)S(1)}, u32[]{:S(2)}, u32[]{:S(2)}) collective-permute-start(s32[1024,128]{1,0:T(8,128)S(1)} %pack.1.refs_0_), channel_id=1, source_target_pairs={{0,2},{1,3},{2,4},{3,5},{4,6},{5,7},{6,0},{7,1},{8,10},{9,11},{10,... | collective-permute-start | bytes 1572872 | tf_op jit(solution)/shard_map/ppermute | solution.py:443
  6.0 14.0 %collective-permute-start.12 = (s32[1024,128]{1,0:T(8,128)S(1)}, s32[1024,128]{1,0:T(8,128)S(1)}, u32[]{:S(2)}, u32[]{:S(2)}) collective-permute-start(s32[1024,128]{1,0:T(8,128)S(1)} %pack.1.refs_0_), channel_id=1, source_target_pairs={{0,8},{1,9},{2,10},{3,11},{4,12},{5,13},{6,14},{7,15},{8,0},{9,1},... | collective-permute-start | bytes 1572872 | tf_op jit(solution)/shard_map/ppermute | solution.py:443
  6.0 15.5 %collective-permute-start.1 = (s32[1024,128]{1,0:T(8,128)S(1)}, s32[1024,128]{1,0:T(8,128)S(1)}, u32[]{:S(2)}, u32[]{:S(2)}) collective-permute-start(s32[1024,128]{1,0:T(8,128)S(1)} %pack.1.refs_0_), channel_id=1, source_target_pairs={{0,16},{1,17},{2,18},{3,19},{4,20},{5,21},{6,22},{7,23},{8,9},{9,8... | collective-permute-start | bytes 1572872 | tf_op jit(solution)/shard_map/ppermute | solution.py:443
  7.5 15.5 %collective-permute-start = (s32[1024,128]{1,0:T(8,128)S(1)}, s32[1024,128]{1,0:T(8,128)S(1)}, u32[]{:S(2)}, u32[]{:S(2)}) collective-permute-start(s32[1024,128]{1,0:T(8,128)S(1)} %pack.1.refs_0_), channel_id=1, source_target_pairs={{0,1},{1,0},{2,3},{3,2},{4,5},{5,4},{6,7},{7,6},{8,24},{9,25},{10,... | collective-permute-start | bytes 1572872 | tf_op jit(solution)/shard_map/ppermute | solution.py:443
  19.9 16.1 %collective-permute-start.7 = (s32[1024,128]{1,0:T(8,128)S(1)}, s32[1024,128]{1,0:T(8,128)S(1)}, u32[]{:S(2)}, u32[]{:S(2)}) collective-permute-start(s32[1024,128]{1,0:T(8,128)S(1)} %collective-permute-done.3.refs_4_), channel_id=1, source_target_pairs={{0,2},{1,3},{2,4},{3,5},{4,6},{5,7},{6,0},{7,1},{8,10},{9,11},{10,... | collective-permute-start | bytes 1572872 | tf_op jit(solution)/shard_map/ppermute | solution.py:443
  19.9 17.6 %collective-permute-start.5 = (s32[1024,128]{1,0:T(8,128)S(1)}, s32[1024,128]{1,0:T(8,128)S(1)}, u32[]{:S(2)}, u32[]{:S(2)}) collective-permute-start(s32[1024,128]{1,0:T(8,128)S(1)} %collective-permute-done.3.refs_4_), channel_id=1, source_target_pairs={{0,16},{1,17},{2,18},{3,19},{4,20},{5,21},{6,22},{7,23},{8,9},{9,8... | collective-permute-start | bytes 1572872 | tf_op jit(solution)/shard_map/ppermute | solution.py:443
  21.5 16.1 %collective-permute-start.4 = (s32[1024,128]{1,0:T(8,128)S(1)}, s32[1024,128]{1,0:T(8,128)S(1)}, u32[]{:S(2)}, u32[]{:S(2)}) collective-permute-start(s32[1024,128]{1,0:T(8,128)S(1)} %collective-permute-done.3.refs_4_), channel_id=1, source_target_pairs={{0,1},{1,0},{2,3},{3,2},{4,5},{5,4},{6,7},{7,6},{8,24},{9,25},{10,... | collective-permute-start | bytes 1572872 | tf_op jit(solution)/shard_map/ppermute | solution.py:443
  23.0 14.6 %collective-permute-start.14 = (s32[1024,128]{1,0:T(8,128)S(1)}, s32[1024,128]{1,0:T(8,128)S(1)}, u32[]{:S(2)}, u32[]{:S(2)}) collective-permute-start(s32[1024,128]{1,0:T(8,128)S(1)} %collective-permute-done.1.refs_2_), channel_id=1, source_target_pairs={{0,8},{1,9},{2,10},{3,11},{4,12},{5,13},{6,14},{7,15},{8,0},{9,1},... | collective-permute-start | bytes 1572872 | tf_op jit(solution)/shard_map/ppermute | solution.py:443
  23.0 15.5 %collective-permute-start.13 = (s32[1024,128]{1,0:T(8,128)S(1)}, s32[1024,128]{1,0:T(8,128)S(1)}, u32[]{:S(2)}, u32[]{:S(2)}) collective-permute-start(s32[1024,128]{1,0:T(8,128)S(1)} %collective-permute-done.refs_1_), channel_id=1, source_target_pairs={{0,8},{1,9},{2,10},{3,11},{4,12},{5,13},{6,14},{7,15},{8,0},{9,1},... | collective-permute-start | bytes 1572872 | tf_op jit(solution)/shard_map/ppermute | solution.py:443
  37.6 16.1 %collective-permute-start.10 = (s32[1024,128]{1,0:T(8,128)S(1)}, s32[1024,128]{1,0:T(8,128)S(1)}, u32[]{:S(2)}, u32[]{:S(2)}) collective-permute-start(s32[1024,128]{1,0:T(8,128)S(1)} %collective-permute-done.7.refs_8_), channel_id=1, source_target_pairs={{0,2},{1,3},{2,4},{3,5},{4,6},{5,7},{6,0},{7,1},{8,10},{9,11},{10,... | collective-permute-start | bytes 1572872 | tf_op jit(solution)/shard_map/ppermute | solution.py:443
  37.7 18.8 %collective-permute-start.9 = (s32[1024,128]{1,0:T(8,128)S(1)}, s32[1024,128]{1,0:T(8,128)S(1)}, u32[]{:S(2)}, u32[]{:S(2)}) collective-permute-start(s32[1024,128]{1,0:T(8,128)S(1)} %collective-permute-done.7.refs_8_), channel_id=1, source_target_pairs={{0,16},{1,17},{2,18},{3,19},{4,20},{5,21},{6,22},{7,23},{8,9},{9,8... | collective-permute-start | bytes 1572872 | tf_op jit(solution)/shard_map/ppermute | solution.py:443
  38.5 18.0 %collective-permute-start.8 = (s32[1024,128]{1,0:T(8,128)S(1)}, s32[1024,128]{1,0:T(8,128)S(1)}, u32[]{:S(2)}, u32[]{:S(2)}) collective-permute-start(s32[1024,128]{1,0:T(8,128)S(1)} %collective-permute-done.7.refs_8_), channel_id=1, source_target_pairs={{0,1},{1,0},{2,3},{3,2},{4,5},{5,4},{6,7},{7,6},{8,24},{9,25},{10,... | collective-permute-start | bytes 1572872 | tf_op jit(solution)/shard_map/ppermute | solution.py:443
  56.5 14.4 %collective-permute-start.6 = (s32[1024,128]{1,0:T(8,128)S(1)}, s32[1024,128]{1,0:T(8,128)S(1)}, u32[]{:S(2)}, u32[]{:S(2)}) collective-permute-start(s32[1024,128]{1,0:T(8,128)S(1)} %collective-permute-done.2.refs_3_), channel_id=1, source_target_pairs={{0,2},{1,3},{2,4},{3,5},{4,6},{5,7},{6,0},{7,1},{8,10},{9,11},{10,... | collective-permute-start | bytes 1572872 | tf_op jit(solution)/shard_map/ppermute | solution.py:443
  56.5 14.4 %collective-permute-start.24 = (s32[1024,128]{1,0:T(8,128)S(1)}, s32[1024,128]{1,0:T(8,128)S(1)}, u32[]{:S(2)}, u32[]{:S(2)}) collective-permute-start(s32[1024,128]{1,0:T(8,128)S(1)} %collective-permute-done.10.refs_11_), channel_id=1, source_target_pairs={{0,16},{1,17},{2,18},{3,19},{4,20},{5,21},{6,22},{7,23},{8,9},{9,8... | collective-permute-start | bytes 1572872 | tf_op jit(solution)/shard_map/ppermute | solution.py:443
  58.0 12.9 %collective-permute-start.11 = (s32[1024,128]{1,0:T(8,128)S(1)}, s32[1024,128]{1,0:T(8,128)S(1)}, u32[]{:S(2)}, u32[]{:S(2)}) collective-permute-start(s32[1024,128]{1,0:T(8,128)S(1)} %collective-permute-done.10.refs_11_), channel_id=1, source_target_pairs={{0,1},{1,0},{2,3},{3,2},{4,5},{5,4},{6,7},{7,6},{8,24},{9,25},{10,... | collective-permute-start | bytes 1572872 | tf_op jit(solution)/shard_map/ppermute | solution.py:443
  59.5 13.0 %collective-permute-start.22 = (s32[1024,128]{1,0:T(8,128)S(1)}, s32[1024,128]{1,0:T(8,128)S(1)}, u32[]{:S(2)}, u32[]{:S(2)}) collective-permute-start(s32[1024,128]{1,0:T(8,128)S(1)} %collective-permute-done.10.refs_11_), channel_id=1, source_target_pairs={{0,8},{1,9},{2,10},{3,11},{4,12},{5,13},{6,14},{7,15},{8,0},{9,1},... | collective-permute-start | bytes 1572872 | tf_op jit(solution)/shard_map/ppermute | solution.py:443
  59.5 13.2 %collective-permute-start.21 = (s32[1024,128]{1,0:T(8,128)S(1)}, s32[1024,128]{1,0:T(8,128)S(1)}, u32[]{:S(2)}, u32[]{:S(2)}) collective-permute-start(s32[1024,128]{1,0:T(8,128)S(1)} %collective-permute-done.9.refs_10_), channel_id=1, source_target_pairs={{0,8},{1,9},{2,10},{3,11},{4,12},{5,13},{6,14},{7,15},{8,0},{9,1},... | collective-permute-start | bytes 1572872 | tf_op jit(solution)/shard_map/ppermute | solution.py:443
  70.9 16.1 %collective-permute-start.23 = (s32[1024,128]{1,0:T(8,128)S(1)}, s32[1024,128]{1,0:T(8,128)S(1)}, u32[]{:S(2)}, u32[]{:S(2)}) collective-permute-start(s32[1024,128]{1,0:T(8,128)S(1)} %collective-permute-done.6.refs_7_), channel_id=1, source_target_pairs={{0,2},{1,3},{2,4},{3,5},{4,6},{5,7},{6,0},{7,1},{8,10},{9,11},{10,... | collective-permute-start | bytes 1572872 | tf_op jit(solution)/shard_map/ppermute | solution.py:443
  70.9 16.1 %collective-permute-start.25 = (s32[1024,128]{1,0:T(8,128)S(1)}, s32[1024,128]{1,0:T(8,128)S(1)}, u32[]{:S(2)}, u32[]{:S(2)}) collective-permute-start(s32[1024,128]{1,0:T(8,128)S(1)} %collective-permute-done.11.refs_12_), channel_id=1, source_target_pairs={{0,16},{1,17},{2,18},{3,19},{4,20},{5,21},{6,22},{7,23},{8,9},{9,8... | collective-permute-start | bytes 1572872 | tf_op jit(solution)/shard_map/ppermute | solution.py:443
  72.5 33.0 %collective-permute-start.26 = (s32[1024,128]{1,0:T(8,128)S(1)}, s32[1024,128]{1,0:T(8,128)S(1)}, u32[]{:S(2)}, u32[]{:S(2)}) collective-permute-start(s32[1024,128]{1,0:T(8,128)S(1)} %collective-permute-done.6.refs_7_), channel_id=1, source_target_pairs={{0,8},{1,9},{2,10},{3,11},{4,12},{5,13},{6,14},{7,15},{8,0},{9,1},... | collective-permute-start | bytes 1572872 | tf_op jit(solution)/shard_map/ppermute | solution.py:443
  72.7 32.8 %collective-permute-start.28 = (s32[1024,128]{1,0:T(8,128)S(1)}, s32[1024,128]{1,0:T(8,128)S(1)}, u32[]{:S(2)}, u32[]{:S(2)}) collective-permute-start(s32[1024,128]{1,0:T(8,128)S(1)} %collective-permute-done.11.refs_12_), channel_id=1, source_target_pairs={{0,8},{1,9},{2,10},{3,11},{4,12},{5,13},{6,14},{7,15},{8,0},{9,1},... | collective-permute-start | bytes 1572872 | tf_op jit(solution)/shard_map/ppermute | solution.py:443
  73.0 32.5 %collective-permute-start.29 = (s32[1024,128]{1,0:T(8,128)S(1)}, s32[1024,128]{1,0:T(8,128)S(1)}, u32[]{:S(2)}, u32[]{:S(2)}) collective-permute-start(s32[1024,128]{1,0:T(8,128)S(1)} %collective-permute-done.24.rest_6_), channel_id=1, source_target_pairs={{0,8},{1,9},{2,10},{3,11},{4,12},{5,13},{6,14},{7,15},{8,0},{9,1},... | collective-permute-start | bytes 1572872 | tf_op jit(solution)/shard_map/ppermute | solution.py:443
  87.0 18.5 %collective-permute-start.27 = (s32[1024,128]{1,0:T(8,128)S(1)}, s32[1024,128]{1,0:T(8,128)S(1)}, u32[]{:S(2)}, u32[]{:S(2)}) collective-permute-start(s32[1024,128]{1,0:T(8,128)S(1)} %collective-permute-done.23.rest_5_), channel_id=1, source_target_pairs={{0,8},{1,9},{2,10},{3,11},{4,12},{5,13},{6,14},{7,15},{8,0},{9,1},... | collective-permute-start | bytes 1572872 | tf_op jit(solution)/shard_map/ppermute | solution.py:443
  87.0 18.5 %collective-permute-start.30 = (s32[1024,128]{1,0:T(8,128)S(1)}, s32[1024,128]{1,0:T(8,128)S(1)}, u32[]{:S(2)}, u32[]{:S(2)}) collective-permute-start(s32[1024,128]{1,0:T(8,128)S(1)} %collective-permute-done.25.rest_7_), channel_id=1, source_target_pairs={{0,8},{1,9},{2,10},{3,11},{4,12},{5,13},{6,14},{7,15},{8,0},{9,1},... | collective-permute-start | bytes 1572872 | tf_op jit(solution)/shard_map/ppermute | solution.py:443
  (18 other events, 303.9 us)

commit v3 on v2

--- a/solution.py
+++ b/solution.py
@@ -14,8 +14,7 @@
 TABLE_LIMIT = 24 * 2**20
 UNIT, WIDEST = float(2**20), 32767.0
 SHARES = (5, 5, 4, 1, 1)
-STAGED = tuple(i for i in range(16) if i not in (11, 14, 15))
-STAGED += tuple(16 + i for i in range(16) if i not in (7, 11, 13, 14, 15))
+STAGED = tuple(i for i in range(32) if i % 16 not in (7, 11, 13, 14, 15))
 
 
 def iota(shape, dim):
@@ -445,6 +444,9 @@
     def ring(y, core, z, x):
         return (y, core, (z + 1) % depth, x)
 
+    def back(y, core, z, x):
+        return (y, core, (z - 1) % depth, x)
+
     def near(y, core, z, x):
         return (y, core, z, x ^ 1) if core == 0 else (y ^ 1, core, z, x)
 
@@ -454,16 +456,13 @@
     def twin(y, core, z, x):
         return (y, 1 - core, z, x)
 
-    start, beside, opposite, diagonal = [block], [], [], []
-    for i in range(depth):
-        if i:
-            start.append(move(start[-1], ring))
-        beside.append(move(start[-1], near))
-        opposite.append(move(start[-1], far))
-        if 0 < i < depth - 1:
-            diagonal.append(move(diagonal[-1], ring))
-        else:
-            diagonal.append(move(beside[-1], far))
+    start = [block, move(block, ring), None, move(block, back)]
+    start[2] = move(start[1], ring)
+    beside = [move(part, near) for part in start]
+    opposite = [move(part, far) for part in start]
+    first = move(beside[0], far)
+    diagonal = [first, move(first, ring), None, move(first, back)]
+    diagonal[2] = move(beside[2], far)
     mine = [part for group in zip(start, beside, opposite, diagonal) for part in group]
     return mine + [move(part, twin) for part in mine]
 

time: 145 us -> 147 us (1.014)
  starting transfers between devices: 22.7 us -> 26.8 us
  waiting for transfers between devices: 71.1 us -> 67.1 us
  blocking collectives: 10.4 us -> 12.7 us
    ppermute x31, starting transfers between devices: 20.2 us -> 24.3 us  [move(): return lax.ppermute(array, AXES, pairs)]
    ppermute x31, waiting for transfers between devices: 64.4 us -> 60.5 us  [move(): return lax.ppermute(array, AXES, pairs)]
    all_to_all x1, blocking collectives: 10.4 us -> 12.7 us  [local(): lax.all_to_all(outgoing_two, AXES, split_axis=0, concat_axis=0, tiled=True)]
  transfers between devices with their start and end apart: 32 -> 32, of which waited for: 8 -> 9; matrix products, arithmetic and copies ran while one was open for 0% -> 0% of each run, Pallas kernels for 9% -> 9%
where the time goes in v3:
time: 147 us
  waiting for transfers between devices  67.1 us (46%)
  Pallas kernels  30.7 us (21%)
  starting transfers between devices  26.8 us (18%)
  blocking collectives  12.7 us (9%)
  local copies, waits for them, and re-layouts  6.37 us (4%)
  between operations  2.68 us (2%)
    ppermute x31, waiting for transfers between devices, move(): return lax.ppermute(array, AXES, pairs)  60.5 us
    ppermute x31, starting transfers between devices, move(): return lax.ppermute(array, AXES, pairs)  24.3 us
    pallas_call x1, Pallas kernels, values_from(): pl.pallas_call(functools.partial(value_body, rest), out_shape=(jax.ShapeD...  15.6 us
    all_to_all x1, blocking collectives, local(): lax.all_to_all(outgoing_two, AXES, split_axis=0, concat_axis=0, tiled=True)  12.7 us
    pallas_call x5, Pallas kernels, lookups(): pl.pallas_call(functools.partial(lookup_body, first, last), out_shape=jax...  9.2 us
    all_to_all x1, waiting for transfers between devices, local(): gaps = lax.all_to_all(gaps, AXES, split_axis=0, concat_axis=0, tiled=True)  6.63 us
    unnamed x20, local copies, waits for them, and re-layouts  5.85 us
    pallas_call x1, Pallas kernels, staged(): pl.pallas_call(functools.partial(stage_body, STAGED, along, width, size),...  3.2 us
  transfers between devices with their start and end apart: 32, of which 9 were waited for; matrix products, arithmetic and copies ran while one was open for 0% of the time, Pallas kernels for 9%

profile of v3, /device:TPU:0, one launch (start us, length us, event | category | flops | bytes accessed | tf_op | source)
XLA Modules:
  0.0 147.0 jit_solution(10267236639625515751)
XLA Ops:
  2.9 5.1 %collective-permute-start.9 = (s32[1024,128]{1,0:T(8,128)S(1)}, s32[1024,128]{1,0:T(8,128)S(1)}, u32[]{:S(2)}, u32[]{:S(2)}) collective-permute-start(s32[1024,128]{1,0:T(8,128)S(1)} %pack.1.refs_0_), channel_id=1, source_target_pairs={{0,6},{1,7},{2,0},{3,1},{4,2},{5,3},{6,4},{7,5},{8,14},{9,15},{10,... | collective-permute-start | bytes 1572872 | tf_op jit(solution)/shard_map/ppermute | solution.py:442
  8.0 1.5 %collective-permute-start.1 = (s32[1024,128]{1,0:T(8,128)S(1)}, s32[1024,128]{1,0:T(8,128)S(1)}, u32[]{:S(2)}, u32[]{:S(2)}) collective-permute-start(s32[1024,128]{1,0:T(8,128)S(1)} %pack.1.refs_0_), channel_id=1, source_target_pairs={{0,16},{1,17},{2,18},{3,19},{4,20},{5,21},{6,22},{7,23},{8,9},{9,8... | collective-permute-start | bytes 1572872 | tf_op jit(solution)/shard_map/ppermute | solution.py:442
  9.5 1.5 %collective-permute-start = (s32[1024,128]{1,0:T(8,128)S(1)}, s32[1024,128]{1,0:T(8,128)S(1)}, u32[]{:S(2)}, u32[]{:S(2)}) collective-permute-start(s32[1024,128]{1,0:T(8,128)S(1)} %pack.1.refs_0_), channel_id=1, source_target_pairs={{0,1},{1,0},{2,3},{3,2},{4,5},{5,4},{6,7},{7,6},{8,24},{9,25},{10,... | collective-permute-start | bytes 1572872 | tf_op jit(solution)/shard_map/ppermute | solution.py:442
  11.0 9.3 %collective-permute-done.9.refs_10_ = s32[1024,128]{1,0:T(8,128)S(1)} collective-permute-done((s32[1024,128]{1,0:T(8,128)S(1)}, s32[1024,128]{1,0:T(8,128)S(1)}, u32[]{:S(2)}, u32[]{:S(2)}) %collective-permute-start.9) | collective-permute-done | bytes 524320 | tf_op jit(solution)/shard_map/ppermute | solution.py:442
  20.3 1.5 %collective-permute-start.24 = (s32[1024,128]{1,0:T(8,128)S(1)}, s32[1024,128]{1,0:T(8,128)S(1)}, u32[]{:S(2)}, u32[]{:S(2)}) collective-permute-start(s32[1024,128]{1,0:T(8,128)S(1)} %collective-permute-done.9.refs_10_), channel_id=1, source_target_pairs={{0,16},{1,17},{2,18},{3,19},{4,20},{5,21},{6,22},{7,23},{8,9},{9,8... | collective-permute-start | bytes 1572872 | tf_op jit(solution)/shard_map/ppermute | solution.py:442
  21.8 1.5 %collective-permute-start.23 = (s32[1024,128]{1,0:T(8,128)S(1)}, s32[1024,128]{1,0:T(8,128)S(1)}, u32[]{:S(2)}, u32[]{:S(2)}) collective-permute-start(s32[1024,128]{1,0:T(8,128)S(1)} %collective-permute-done.9.refs_10_), channel_id=1, source_target_pairs={{0,1},{1,0},{2,3},{3,2},{4,5},{5,4},{6,7},{7,6},{8,24},{9,25},{10,... | collective-permute-start | bytes 1572872 | tf_op jit(solution)/shard_map/ppermute | solution.py:442
  23.3 8.0 %collective-permute-done.3.refs_4_ = s32[1024,128]{1,0:T(8,128)S(1)} collective-permute-done((s32[1024,128]{1,0:T(8,128)S(1)}, s32[1024,128]{1,0:T(8,128)S(1)}, u32[]{:S(2)}, u32[]{:S(2)}) %collective-permute-start.3) | collective-permute-done | bytes 524320 | tf_op jit(solution)/shard_map/ppermute | solution.py:442
  31.8 1.6 %collective-permute-start.6 = (s32[1024,128]{1,0:T(8,128)S(1)}, s32[1024,128]{1,0:T(8,128)S(1)}, u32[]{:S(2)}, u32[]{:S(2)}) collective-permute-start(s32[1024,128]{1,0:T(8,128)S(1)} %collective-permute-done.3.refs_4_), channel_id=1, source_target_pairs={{0,2},{1,3},{2,4},{3,5},{4,6},{5,7},{6,0},{7,1},{8,10},{9,11},{10,... | collective-permute-start | bytes 1572872 | tf_op jit(solution)/shard_map/ppermute | solution.py:442
  34.0 1.5 %collective-permute-start.5 = (s32[1024,128]{1,0:T(8,128)S(1)}, s32[1024,128]{1,0:T(8,128)S(1)}, u32[]{:S(2)}, u32[]{:S(2)}) collective-permute-start(s32[1024,128]{1,0:T(8,128)S(1)} %collective-permute-done.3.refs_4_), channel_id=1, source_target_pairs={{0,16},{1,17},{2,18},{3,19},{4,20},{5,21},{6,22},{7,23},{8,9},{9,8... | collective-permute-start | bytes 1572872 | tf_op jit(solution)/shard_map/ppermute | solution.py:442
  37.4 10.2 %collective-permute-done.6.refs_7_ = s32[1024,128]{1,0:T(8,128)S(1)} collective-permute-done((s32[1024,128]{1,0:T(8,128)S(1)}, s32[1024,128]{1,0:T(8,128)S(1)}, u32[]{:S(2)}, u32[]{:S(2)}) %collective-permute-start.6) | collective-permute-done | bytes 524320 | tf_op jit(solution)/shard_map/ppermute | solution.py:442
  47.5 1.5 %collective-permute-start.2 = (s32[1024,128]{1,0:T(8,128)S(1)}, s32[1024,128]{1,0:T(8,128)S(1)}, u32[]{:S(2)}, u32[]{:S(2)}) collective-permute-start(s32[1024,128]{1,0:T(8,128)S(1)} %collective-permute-done.refs_1_), channel_id=1, source_target_pairs={{0,16},{1,17},{2,18},{3,19},{4,20},{5,21},{6,22},{7,23},{8,9},{9,8... | collective-permute-start | bytes 1572872 | tf_op jit(solution)/shard_map/ppermute | solution.py:442
  49.8 1.3 collective-permute-start.7
  51.1 9.0 %collective-permute-done.2.refs_3_ = s32[1024,128]{1,0:T(8,128)S(1)} collective-permute-done((s32[1024,128]{1,0:T(8,128)S(1)}, s32[1024,128]{1,0:T(8,128)S(1)}, u32[]{:S(2)}, u32[]{:S(2)}) %collective-permute-start.2) | collective-permute-done | bytes 524320 | tf_op jit(solution)/shard_map/ppermute | solution.py:442
  61.0 7.0 %collective-permute-done.8.refs_9_ = s32[1024,128]{1,0:T(8,128)S(1)} collective-permute-done((s32[1024,128]{1,0:T(8,128)S(1)}, s32[1024,128]{1,0:T(8,128)S(1)}, u32[]{:S(2)}, u32[]{:S(2)}) %collective-permute-start.8) | collective-permute-done | bytes 524320 | tf_op jit(solution)/shard_map/ppermute | solution.py:442
  68.5 1.5 %collective-permute-start.22 = (s32[1024,128]{1,0:T(8,128)S(1)}, s32[1024,128]{1,0:T(8,128)S(1)}, u32[]{:S(2)}, u32[]{:S(2)}) collective-permute-start(s32[1024,128]{1,0:T(8,128)S(1)} %collective-permute-done.7.refs_8_), channel_id=1, source_target_pairs={{0,16},{1,17},{2,18},{3,19},{4,20},{5,21},{6,22},{7,23},{8,9},{9,8... | collective-permute-start | bytes 1572872 | tf_op jit(solution)/shard_map/ppermute | solution.py:442
  70.0 15.7 %collective-permute-done.25.rest_9_ = s32[1024,128]{1,0:T(8,128)S(1)} collective-permute-done((s32[1024,128]{1,0:T(8,128)S(1)}, s32[1024,128]{1,0:T(8,128)S(1)}, u32[]{:S(2)}, u32[]{:S(2)}) %collective-permute-start.25) | collective-permute-done | bytes 524320 | tf_op jit(solution)/shard_map/ppermute | solution.py:442
  89.7 2.9 %lookup.5.refs_0_ = s32[128,128]{1,0:T(8,128)S(1)} custom-call(bf16[256,512]{1,0:T(8,128)(2,1)S(1)} %planes.1.planes_ref, s32[128,128]{1,0:T(8,128)S(1)} %bitcast.16), custom_call_target="tpu_custom_call" | custom-call | tf_op jit(solution)/shard_map/lookup/pallas_call | solution.py:103
  93.4 2.9 %lookup.6.refs_0_ = s32[128,128]{1,0:T(8,128)S(1)} custom-call(bf16[256,512]{1,0:T(8,128)(2,1)S(1)} %planes.1.planes_ref, s32[128,128]{1,0:T(8,128)S(1)} %bitcast.17, s32[128,128]{1,0:T(8,128)S(1)} %lookup.5.refs_0_), custom_call_target="tpu_custom_call" | custom-call | tf_op jit(solution)/shard_map/lookup/pallas_call | solution.py:103
  96.3 2.3 %lookup.7.refs_0_ = s32[128,128]{1,0:T(8,128)S(1)} custom-call(bf16[256,512]{1,0:T(8,128)(2,1)S(1)} %planes.1.planes_ref, s32[128,128]{1,0:T(8,128)S(1)} %bitcast.18, s32[128,128]{1,0:T(8,128)S(1)} %lookup.6.refs_0_), custom_call_target="tpu_custom_call" | custom-call | tf_op jit(solution)/shard_map/lookup/pallas_call | solution.py:103
  102.3 3.2 %stage.1 = (s32[32784,128]{1,0:T(8,128)S(1)}, s32[128,128]{1,0:T(8,128)S(1)}, s32[128,128]{1,0:T(8,128)S(1)}, bf16[16384,128]{1,0:T(8,128)(2,1)S(1)}) custom-call(s32[128,128]{1,0:T(8,128)S(1)} %lookup.9.home_ref, bf16[16384,128]{1,0:T(8,128)(2,1)} %child_ref.1, s32[1024,128]{1,0:T(8,128)S(1)} %pack.1.refs_0_, s32[1024,128]{1,0:T(8,128)S(1)} %collective-permute-done.refs_1_, ...), custom_call_target="tpu_custom_call" | custom-call | tf_op jit(solution)/shard_map/stage/pallas_call | solution.py:238
  105.6 15.6 %values.1 = (f32[128,128]{1,0:T(8,128)}, s32[32,8,128]{2,1,0:T(8,128)S(1)}, s32[32784,128]{1,0:T(8,128)S(1)}) custom-call(s32[16384]{0:T(1024)S(1)} %bitcast.23, s32[128,128]{1,0:T(8,128)S(1)} %get-tuple-element.15.odd_ref, bf16[16384,128]{1,0:T(8,128)(2,1)S(1)} %get-tuple-element.16.child, ...), custom_call_target="tpu_custom_call", output_to_operand_aliasing={{2}: (7, {})} | custom-call | tf_op jit(solution)/shard_map/values/pallas_call | solution.py:306
  121.2 12.7 %all_to_all.17.incoming_ref = s32[32,8,128]{2,1,0:T(8,128)S(1)} all-to-all(s32[32,8,128]{2,1,0:T(8,128)S(1)} %get-tuple-element.21), channel_id=1, replica_groups=mesh['gx'=4,'gy'=8] {'gx','gy'}, dimensions={0} | all-to-all | bytes 262144 | tf_op jit(solution)/shard_map/all_to_all | solution.py:505
  135.0 2.5 %all-to-all-start.1 = ((f32[32,1,128]{2,1,0:T(1,128)}), f32[32,1,128]{2,1,0:T(1,128)S(1)}, u32[]{:S(2)}, u32[]{:S(2)}) async-start(f32[32,1,128]{2,1,0:T(1,128)} %bitcast.10), calls=%async_computation.1 | async-start | bytes 32768 | tf_op jit(solution)/shard_map/all_to_all | solution.py:508
  138.0 6.6 %all-to-all-done.1 = f32[32,1,128]{2,1,0:T(1,128)S(1)} async-done(((f32[32,1,128]{2,1,0:T(1,128)}), f32[32,1,128]{2,1,0:T(1,128)S(1)}, u32[]{:S(2)}, u32[]{:S(2)}) %all-to-all-start.1) | async-done | bytes 16416 | tf_op jit(solution)/shard_map/all_to_all | solution.py:508
  (74 shorter events, 17.9 us)
Async XLA Ops:
  2.9 17.4 %collective-permute-start.9 = (s32[1024,128]{1,0:T(8,128)S(1)}, s32[1024,128]{1,0:T(8,128)S(1)}, u32[]{:S(2)}, u32[]{:S(2)}) collective-permute-start(s32[1024,128]{1,0:T(8,128)S(1)} %pack.1.refs_0_), channel_id=1, source_target_pairs={{0,6},{1,7},{2,0},{3,1},{4,2},{5,3},{6,4},{7,5},{8,14},{9,15},{10,... | collective-permute-start | bytes 1572872 | tf_op jit(solution)/shard_map/ppermute | solution.py:442
  8.0 13.8 %collective-permute-start.10 = (s32[1024,128]{1,0:T(8,128)S(1)}, s32[1024,128]{1,0:T(8,128)S(1)}, u32[]{:S(2)}, u32[]{:S(2)}) collective-permute-start(s32[1024,128]{1,0:T(8,128)S(1)} %pack.1.refs_0_), channel_id=1, source_target_pairs={{0,8},{1,9},{2,10},{3,11},{4,12},{5,13},{6,14},{7,15},{8,0},{9,1},... | collective-permute-start | bytes 1572872 | tf_op jit(solution)/shard_map/ppermute | solution.py:442
  8.0 23.3 %collective-permute-start.3 = (s32[1024,128]{1,0:T(8,128)S(1)}, s32[1024,128]{1,0:T(8,128)S(1)}, u32[]{:S(2)}, u32[]{:S(2)}) collective-permute-start(s32[1024,128]{1,0:T(8,128)S(1)} %pack.1.refs_0_), channel_id=1, source_target_pairs={{0,2},{1,3},{2,4},{3,5},{4,6},{5,7},{6,0},{7,1},{8,10},{9,11},{10,... | collective-permute-start | bytes 1572872 | tf_op jit(solution)/shard_map/ppermute | solution.py:442
  8.0 23.3 %collective-permute-start.1 = (s32[1024,128]{1,0:T(8,128)S(1)}, s32[1024,128]{1,0:T(8,128)S(1)}, u32[]{:S(2)}, u32[]{:S(2)}) collective-permute-start(s32[1024,128]{1,0:T(8,128)S(1)} %pack.1.refs_0_), channel_id=1, source_target_pairs={{0,16},{1,17},{2,18},{3,19},{4,20},{5,21},{6,22},{7,23},{8,9},{9,8... | collective-permute-start | bytes 1572872 | tf_op jit(solution)/shard_map/ppermute | solution.py:442
  9.5 22.3 %collective-permute-start = (s32[1024,128]{1,0:T(8,128)S(1)}, s32[1024,128]{1,0:T(8,128)S(1)}, u32[]{:S(2)}, u32[]{:S(2)}) collective-permute-start(s32[1024,128]{1,0:T(8,128)S(1)} %pack.1.refs_0_), channel_id=1, source_target_pairs={{0,1},{1,0},{2,3},{3,2},{4,5},{5,4},{6,7},{7,6},{8,24},{9,25},{10,... | collective-permute-start | bytes 1572872 | tf_op jit(solution)/shard_map/ppermute | solution.py:442
  20.3 13.7 %collective-permute-start.24 = (s32[1024,128]{1,0:T(8,128)S(1)}, s32[1024,128]{1,0:T(8,128)S(1)}, u32[]{:S(2)}, u32[]{:S(2)}) collective-permute-start(s32[1024,128]{1,0:T(8,128)S(1)} %collective-permute-done.9.refs_10_), channel_id=1, source_target_pairs={{0,16},{1,17},{2,18},{3,19},{4,20},{5,21},{6,22},{7,23},{8,9},{9,8... | collective-permute-start | bytes 1572872 | tf_op jit(solution)/shard_map/ppermute | solution.py:442
  21.8 13.7 %collective-permute-start.23 = (s32[1024,128]{1,0:T(8,128)S(1)}, s32[1024,128]{1,0:T(8,128)S(1)}, u32[]{:S(2)}, u32[]{:S(2)}) collective-permute-start(s32[1024,128]{1,0:T(8,128)S(1)} %collective-permute-done.9.refs_10_), channel_id=1, source_target_pairs={{0,1},{1,0},{2,3},{3,2},{4,5},{5,4},{6,7},{7,6},{8,24},{9,25},{10,... | collective-permute-start | bytes 1572872 | tf_op jit(solution)/shard_map/ppermute | solution.py:442
  31.8 15.7 %collective-permute-start.6 = (s32[1024,128]{1,0:T(8,128)S(1)}, s32[1024,128]{1,0:T(8,128)S(1)}, u32[]{:S(2)}, u32[]{:S(2)}) collective-permute-start(s32[1024,128]{1,0:T(8,128)S(1)} %collective-permute-done.3.refs_4_), channel_id=1, source_target_pairs={{0,2},{1,3},{2,4},{3,5},{4,6},{5,7},{6,0},{7,1},{8,10},{9,11},{10,... | collective-permute-start | bytes 1572872 | tf_op jit(solution)/shard_map/ppermute | solution.py:442
  34.0 15.0 %collective-permute-start.5 = (s32[1024,128]{1,0:T(8,128)S(1)}, s32[1024,128]{1,0:T(8,128)S(1)}, u32[]{:S(2)}, u32[]{:S(2)}) collective-permute-start(s32[1024,128]{1,0:T(8,128)S(1)} %collective-permute-done.3.refs_4_), channel_id=1, source_target_pairs={{0,16},{1,17},{2,18},{3,19},{4,20},{5,21},{6,22},{7,23},{8,9},{9,8... | collective-permute-start | bytes 1572872 | tf_op jit(solution)/shard_map/ppermute | solution.py:442
  35.6 13.5 %collective-permute-start.4 = (s32[1024,128]{1,0:T(8,128)S(1)}, s32[1024,128]{1,0:T(8,128)S(1)}, u32[]{:S(2)}, u32[]{:S(2)}) collective-permute-start(s32[1024,128]{1,0:T(8,128)S(1)} %collective-permute-done.3.refs_4_), channel_id=1, source_target_pairs={{0,1},{1,0},{2,3},{3,2},{4,5},{5,4},{6,7},{7,6},{8,24},{9,25},{10,... | collective-permute-start | bytes 1572872 | tf_op jit(solution)/shard_map/ppermute | solution.py:442
  36.9 14.3 %collective-permute-start.11 = (s32[1024,128]{1,0:T(8,128)S(1)}, s32[1024,128]{1,0:T(8,128)S(1)}, u32[]{:S(2)}, u32[]{:S(2)}) collective-permute-start(s32[1024,128]{1,0:T(8,128)S(1)} %collective-permute-done.refs_1_), channel_id=1, source_target_pairs={{0,8},{1,9},{2,10},{3,11},{4,12},{5,13},{6,14},{7,15},{8,0},{9,1},... | collective-permute-start | bytes 1572872 | tf_op jit(solution)/shard_map/ppermute | solution.py:442
  49.1 18.9 %collective-permute-start.8 = (s32[1024,128]{1,0:T(8,128)S(1)}, s32[1024,128]{1,0:T(8,128)S(1)}, u32[]{:S(2)}, u32[]{:S(2)}) collective-permute-start(s32[1024,128]{1,0:T(8,128)S(1)} %collective-permute-done.6.refs_7_), channel_id=1, source_target_pairs={{0,16},{1,17},{2,18},{3,19},{4,20},{5,21},{6,22},{7,23},{8,9},{9,8... | collective-permute-start | bytes 1572872 | tf_op jit(solution)/shard_map/ppermute | solution.py:442
  49.8 18.1 %collective-permute-start.7 = (s32[1024,128]{1,0:T(8,128)S(1)}, s32[1024,128]{1,0:T(8,128)S(1)}, u32[]{:S(2)}, u32[]{:S(2)}) collective-permute-start(s32[1024,128]{1,0:T(8,128)S(1)} %collective-permute-done.6.refs_7_), channel_id=1, source_target_pairs={{0,1},{1,0},{2,3},{3,2},{4,5},{5,4},{6,7},{7,6},{8,24},{9,25},{10,... | collective-permute-start | bytes 1572872 | tf_op jit(solution)/shard_map/ppermute | solution.py:442
  51.1 16.8 %collective-permute-start.16 = (s32[1024,128]{1,0:T(8,128)S(1)}, s32[1024,128]{1,0:T(8,128)S(1)}, u32[]{:S(2)}, u32[]{:S(2)}) collective-permute-start(s32[1024,128]{1,0:T(8,128)S(1)} %collective-permute-done.5.refs_6_), channel_id=1, source_target_pairs={{0,8},{1,9},{2,10},{3,11},{4,12},{5,13},{6,14},{7,15},{8,0},{9,1},... | collective-permute-start | bytes 1572872 | tf_op jit(solution)/shard_map/ppermute | solution.py:442
  60.1 25.6 %collective-permute-start.25 = (s32[1024,128]{1,0:T(8,128)S(1)}, s32[1024,128]{1,0:T(8,128)S(1)}, u32[]{:S(2)}, u32[]{:S(2)}) collective-permute-start(s32[1024,128]{1,0:T(8,128)S(1)} %collective-permute-done.2.refs_3_), channel_id=1, source_target_pairs={{0,6},{1,7},{2,0},{3,1},{4,2},{5,3},{6,4},{7,5},{8,14},{9,15},{10,... | collective-permute-start | bytes 1572872 | tf_op jit(solution)/shard_map/ppermute | solution.py:442
  67.9 17.7 %collective-permute-start.21 = (s32[1024,128]{1,0:T(8,128)S(1)}, s32[1024,128]{1,0:T(8,128)S(1)}, u32[]{:S(2)}, u32[]{:S(2)}) collective-permute-start(s32[1024,128]{1,0:T(8,128)S(1)} %collective-permute-done.2.refs_3_), channel_id=1, source_target_pairs={{0,2},{1,3},{2,4},{3,5},{4,6},{5,7},{6,0},{7,1},{8,10},{9,11},{10,... | collective-permute-start | bytes 1572872 | tf_op jit(solution)/shard_map/ppermute | solution.py:442
  68.0 18.2 %collective-permute-start.13 = (s32[1024,128]{1,0:T(8,128)S(1)}, s32[1024,128]{1,0:T(8,128)S(1)}, u32[]{:S(2)}, u32[]{:S(2)}) collective-permute-start(s32[1024,128]{1,0:T(8,128)S(1)} %collective-permute-done.2.refs_3_), channel_id=1, source_target_pairs={{0,8},{1,9},{2,10},{3,11},{4,12},{5,13},{6,14},{7,15},{8,0},{9,1},... | collective-permute-start | bytes 1572872 | tf_op jit(solution)/shard_map/ppermute | solution.py:442
  68.0 18.3 %collective-permute-start.19 = (s32[1024,128]{1,0:T(8,128)S(1)}, s32[1024,128]{1,0:T(8,128)S(1)}, u32[]{:S(2)}, u32[]{:S(2)}) collective-permute-start(s32[1024,128]{1,0:T(8,128)S(1)} %collective-permute-done.8.refs_9_), channel_id=1, source_target_pairs={{0,8},{1,9},{2,10},{3,11},{4,12},{5,13},{6,14},{7,15},{8,0},{9,1},... | collective-permute-start | bytes 1572872 | tf_op jit(solution)/shard_map/ppermute | solution.py:442
  68.5 18.2 %collective-permute-start.22 = (s32[1024,128]{1,0:T(8,128)S(1)}, s32[1024,128]{1,0:T(8,128)S(1)}, u32[]{:S(2)}, u32[]{:S(2)}) collective-permute-start(s32[1024,128]{1,0:T(8,128)S(1)} %collective-permute-done.7.refs_8_), channel_id=1, source_target_pairs={{0,16},{1,17},{2,18},{3,19},{4,20},{5,21},{6,22},{7,23},{8,9},{9,8... | collective-permute-start | bytes 1572872 | tf_op jit(solution)/shard_map/ppermute | solution.py:442
  85.7 19.9 %collective-permute-start.29 = (s32[1024,128]{1,0:T(8,128)S(1)}, s32[1024,128]{1,0:T(8,128)S(1)}, u32[]{:S(2)}, u32[]{:S(2)}) collective-permute-start(s32[1024,128]{1,0:T(8,128)S(1)} %collective-permute-done.24.rest_8_), channel_id=1, source_target_pairs={{0,8},{1,9},{2,10},{3,11},{4,12},{5,13},{6,14},{7,15},{8,0},{9,1},... | collective-permute-start | bytes 1572872 | tf_op jit(solution)/shard_map/ppermute | solution.py:442
  86.2 19.4 %collective-permute-start.28 = (s32[1024,128]{1,0:T(8,128)S(1)}, s32[1024,128]{1,0:T(8,128)S(1)}, u32[]{:S(2)}, u32[]{:S(2)}) collective-permute-start(s32[1024,128]{1,0:T(8,128)S(1)} %collective-permute-done.23.rest_7_), channel_id=1, source_target_pairs={{0,8},{1,9},{2,10},{3,11},{4,12},{5,13},{6,14},{7,15},{8,0},{9,1},... | collective-permute-start | bytes 1572872 | tf_op jit(solution)/shard_map/ppermute | solution.py:442
  86.3 19.3 %collective-permute-start.30 = (s32[1024,128]{1,0:T(8,128)S(1)}, s32[1024,128]{1,0:T(8,128)S(1)}, u32[]{:S(2)}, u32[]{:S(2)}) collective-permute-start(s32[1024,128]{1,0:T(8,128)S(1)} %collective-permute-done.25.rest_9_), channel_id=1, source_target_pairs={{0,8},{1,9},{2,10},{3,11},{4,12},{5,13},{6,14},{7,15},{8,0},{9,1},... | collective-permute-start | bytes 1572872 | tf_op jit(solution)/shard_map/ppermute | solution.py:442
  86.7 18.9 %collective-permute-start.26 = (s32[1024,128]{1,0:T(8,128)S(1)}, s32[1024,128]{1,0:T(8,128)S(1)}, u32[]{:S(2)}, u32[]{:S(2)}) collective-permute-start(s32[1024,128]{1,0:T(8,128)S(1)} %collective-permute-done.21.rest_5_), channel_id=1, source_target_pairs={{0,8},{1,9},{2,10},{3,11},{4,12},{5,13},{6,14},{7,15},{8,0},{9,1},... | collective-permute-start | bytes 1572872 | tf_op jit(solution)/shard_map/ppermute | solution.py:442
  87.6 18.0 %collective-permute-start.27 = (s32[1024,128]{1,0:T(8,128)S(1)}, s32[1024,128]{1,0:T(8,128)S(1)}, u32[]{:S(2)}, u32[]{:S(2)}) collective-permute-start(s32[1024,128]{1,0:T(8,128)S(1)} %collective-permute-done.22.rest_6_), channel_id=1, source_target_pairs={{0,8},{1,9},{2,10},{3,11},{4,12},{5,13},{6,14},{7,15},{8,0},{9,1},... | collective-permute-start | bytes 1572872 | tf_op jit(solution)/shard_map/ppermute | solution.py:442
  (18 other events, 309.4 us)

commit v4 on v3

--- a/solution.py
+++ b/solution.py
@@ -110,9 +110,15 @@
     return found[0]
 
 
-def pack_body(cum_ref, out_ref):
+def pack_body(source_ref, out_ref, cum_ref, sems):
     half = out_ref.shape[0]
-    rows = min(half, 64)
+    parts = sems.shape[0] // 2
+    chunk = half // parts
+    rows = min(chunk, 64)
+
+    def arrival(i):
+        at = pl.ds(half * (i % 2) + chunk * (i // 2), chunk)
+        return pltpu.make_async_copy(source_ref.at[at, :], cum_ref.at[at, :], sems.at[i])
 
     def fixed(first):
         cum = cum_ref[pl.ds(first, rows), :]
@@ -120,11 +126,17 @@
         return (policy.astype(jnp.float32) * float(2**SCALE_BITS) + 0.5).astype(jnp.int32)
 
     def step(i, carry):
-        first = pl.multiple_of(i * rows, rows)
+        first = i * rows
         out_ref[pl.ds(first, rows), :] = fixed(first) | (fixed(first + half) << 16)
         return carry
 
-    lax.fori_loop(0, half // rows, step, 0, unroll=2)
+    for i in range(2 * parts):
+        arrival(i).start()
+    for c in range(parts):
+        arrival(2 * c).wait()
+        arrival(2 * c + 1).wait()
+        for i in range(chunk // rows):
+            step(c * (chunk // rows) + i, 0)
 
 
 def pack(opp_cum):
@@ -132,9 +144,14 @@
     return pl.pallas_call(
         pack_body,
         out_shape=jax.ShapeDtypeStruct((rows // 2, acts), jnp.int32),
+        in_specs=[pl.BlockSpec(memory_space=pltpu.HBM)],
+        scratch_shapes=[
+            pltpu.VMEM((rows, acts), jnp.float32),
+            pltpu.SemaphoreType.DMA((8,)),
+        ],
         compiler_params=room(opp_cum.size * 6),
         name="pack",
-    )(opp_cum)
+    )(pltpu.with_memory_space_constraint(opp_cum, pltpu.HBM))
 
 
 def split(x, parts):

time: 147 us -> 147 us (level)
    unnamed x20 -> x18, local copies, waits for them, and re-layouts: 5.85 us -> 4.64 us
where the time goes in v4:
time: 147 us
  waiting for transfers between devices  67.1 us (46%)
  Pallas kernels  31.5 us (21%)
  starting transfers between devices  26.8 us (18%)
  blocking collectives  12.7 us (9%)
  local copies, waits for them, and re-layouts  5.15 us (4%)
  between operations  2.68 us (2%)
    ppermute x31, waiting for transfers between devices, move(): return lax.ppermute(array, AXES, pairs)  60.5 us
    ppermute x31, starting transfers between devices, move(): return lax.ppermute(array, AXES, pairs)  24.3 us
    pallas_call x1, Pallas kernels, values_from(): pl.pallas_call(functools.partial(value_body, rest), out_shape=(jax.ShapeD...  15.6 us
    all_to_all x1, blocking collectives, local(): lax.all_to_all(outgoing_two, AXES, split_axis=0, concat_axis=0, tiled=True)  12.7 us
    pallas_call x5, Pallas kernels, lookups(): pl.pallas_call(functools.partial(lookup_body, first, last), out_shape=jax...  9.2 us
    all_to_all x1, waiting for transfers between devices, local(): gaps = lax.all_to_all(gaps, AXES, split_axis=0, concat_axis=0, tiled=True)  6.63 us
    unnamed x18, local copies, waits for them, and re-layouts  4.64 us
    pallas_call x1, Pallas kernels, staged(): pl.pallas_call(functools.partial(stage_body, STAGED, along, width, size),...  3.2 us
  transfers between devices with their start and end apart: 32, of which 9 were waited for; matrix products, arithmetic and copies ran while one was open for 0% of the time, Pallas kernels for 9%

profile of v4, /device:TPU:0, one launch (start us, length us, event | category | flops | bytes accessed | tf_op | source)
XLA Modules:
  0.0 146.6 jit_solution(6363156236001834715)
XLA Ops:
  0.7 1.7 %pack.1.refs_0_ = s32[1024,128]{1,0:T(8,128)S(1)} custom-call(f32[2048,128]{1,0:T(8,128)} %source_ref.1), custom_call_target="tpu_custom_call" | custom-call | tf_op jit(solution)/shard_map/pack/pallas_call | solution.py:144
  2.4 5.1 %collective-permute-start.9 = (s32[1024,128]{1,0:T(8,128)S(1)}, s32[1024,128]{1,0:T(8,128)S(1)}, u32[]{:S(2)}, u32[]{:S(2)}) collective-permute-start(s32[1024,128]{1,0:T(8,128)S(1)} %pack.1.refs_0_), channel_id=1, source_target_pairs={{0,6},{1,7},{2,0},{3,1},{4,2},{5,3},{6,4},{7,5},{8,14},{9,15},{10,... | collective-permute-start | bytes 1572872 | tf_op jit(solution)/shard_map/ppermute | solution.py:459
  7.5 1.5 %collective-permute-start.1 = (s32[1024,128]{1,0:T(8,128)S(1)}, s32[1024,128]{1,0:T(8,128)S(1)}, u32[]{:S(2)}, u32[]{:S(2)}) collective-permute-start(s32[1024,128]{1,0:T(8,128)S(1)} %pack.1.refs_0_), channel_id=1, source_target_pairs={{0,16},{1,17},{2,18},{3,19},{4,20},{5,21},{6,22},{7,23},{8,9},{9,8... | collective-permute-start | bytes 1572872 | tf_op jit(solution)/shard_map/ppermute | solution.py:459
  9.1 1.5 %collective-permute-start = (s32[1024,128]{1,0:T(8,128)S(1)}, s32[1024,128]{1,0:T(8,128)S(1)}, u32[]{:S(2)}, u32[]{:S(2)}) collective-permute-start(s32[1024,128]{1,0:T(8,128)S(1)} %pack.1.refs_0_), channel_id=1, source_target_pairs={{0,1},{1,0},{2,3},{3,2},{4,5},{5,4},{6,7},{7,6},{8,24},{9,25},{10,... | collective-permute-start | bytes 1572872 | tf_op jit(solution)/shard_map/ppermute | solution.py:459
  10.5 9.3 %collective-permute-done.9.refs_10_ = s32[1024,128]{1,0:T(8,128)S(1)} collective-permute-done((s32[1024,128]{1,0:T(8,128)S(1)}, s32[1024,128]{1,0:T(8,128)S(1)}, u32[]{:S(2)}, u32[]{:S(2)}) %collective-permute-start.9) | collective-permute-done | bytes 524320 | tf_op jit(solution)/shard_map/ppermute | solution.py:459
  19.8 1.5 %collective-permute-start.24 = (s32[1024,128]{1,0:T(8,128)S(1)}, s32[1024,128]{1,0:T(8,128)S(1)}, u32[]{:S(2)}, u32[]{:S(2)}) collective-permute-start(s32[1024,128]{1,0:T(8,128)S(1)} %collective-permute-done.9.refs_10_), channel_id=1, source_target_pairs={{0,16},{1,17},{2,18},{3,19},{4,20},{5,21},{6,22},{7,23},{8,9},{9,8... | collective-permute-start | bytes 1572872 | tf_op jit(solution)/shard_map/ppermute | solution.py:459
  21.4 1.5 %collective-permute-start.23 = (s32[1024,128]{1,0:T(8,128)S(1)}, s32[1024,128]{1,0:T(8,128)S(1)}, u32[]{:S(2)}, u32[]{:S(2)}) collective-permute-start(s32[1024,128]{1,0:T(8,128)S(1)} %collective-permute-done.9.refs_10_), channel_id=1, source_target_pairs={{0,1},{1,0},{2,3},{3,2},{4,5},{5,4},{6,7},{7,6},{8,24},{9,25},{10,... | collective-permute-start | bytes 1572872 | tf_op jit(solution)/shard_map/ppermute | solution.py:459
  22.9 8.0 %collective-permute-done.3.refs_4_ = s32[1024,128]{1,0:T(8,128)S(1)} collective-permute-done((s32[1024,128]{1,0:T(8,128)S(1)}, s32[1024,128]{1,0:T(8,128)S(1)}, u32[]{:S(2)}, u32[]{:S(2)}) %collective-permute-start.3) | collective-permute-done | bytes 524320 | tf_op jit(solution)/shard_map/ppermute | solution.py:459
  31.4 1.6 %collective-permute-start.6 = (s32[1024,128]{1,0:T(8,128)S(1)}, s32[1024,128]{1,0:T(8,128)S(1)}, u32[]{:S(2)}, u32[]{:S(2)}) collective-permute-start(s32[1024,128]{1,0:T(8,128)S(1)} %collective-permute-done.3.refs_4_), channel_id=1, source_target_pairs={{0,2},{1,3},{2,4},{3,5},{4,6},{5,7},{6,0},{7,1},{8,10},{9,11},{10,... | collective-permute-start | bytes 1572872 | tf_op jit(solution)/shard_map/ppermute | solution.py:459
  33.6 1.5 %collective-permute-start.5 = (s32[1024,128]{1,0:T(8,128)S(1)}, s32[1024,128]{1,0:T(8,128)S(1)}, u32[]{:S(2)}, u32[]{:S(2)}) collective-permute-start(s32[1024,128]{1,0:T(8,128)S(1)} %collective-permute-done.3.refs_4_), channel_id=1, source_target_pairs={{0,16},{1,17},{2,18},{3,19},{4,20},{5,21},{6,22},{7,23},{8,9},{9,8... | collective-permute-start | bytes 1572872 | tf_op jit(solution)/shard_map/ppermute | solution.py:459
  36.9 10.2 %collective-permute-done.6.refs_7_ = s32[1024,128]{1,0:T(8,128)S(1)} collective-permute-done((s32[1024,128]{1,0:T(8,128)S(1)}, s32[1024,128]{1,0:T(8,128)S(1)}, u32[]{:S(2)}, u32[]{:S(2)}) %collective-permute-start.6) | collective-permute-done | bytes 524320 | tf_op jit(solution)/shard_map/ppermute | solution.py:459
  47.0 1.5 %collective-permute-start.2 = (s32[1024,128]{1,0:T(8,128)S(1)}, s32[1024,128]{1,0:T(8,128)S(1)}, u32[]{:S(2)}, u32[]{:S(2)}) collective-permute-start(s32[1024,128]{1,0:T(8,128)S(1)} %collective-permute-done.refs_1_), channel_id=1, source_target_pairs={{0,16},{1,17},{2,18},{3,19},{4,20},{5,21},{6,22},{7,23},{8,9},{9,8... | collective-permute-start | bytes 1572872 | tf_op jit(solution)/shard_map/ppermute | solution.py:459
  50.7 9.0 %collective-permute-done.2.refs_3_ = s32[1024,128]{1,0:T(8,128)S(1)} collective-permute-done((s32[1024,128]{1,0:T(8,128)S(1)}, s32[1024,128]{1,0:T(8,128)S(1)}, u32[]{:S(2)}, u32[]{:S(2)}) %collective-permute-start.2) | collective-permute-done | bytes 524320 | tf_op jit(solution)/shard_map/ppermute | solution.py:459
  60.5 7.0 %collective-permute-done.8.refs_9_ = s32[1024,128]{1,0:T(8,128)S(1)} collective-permute-done((s32[1024,128]{1,0:T(8,128)S(1)}, s32[1024,128]{1,0:T(8,128)S(1)}, u32[]{:S(2)}, u32[]{:S(2)}) %collective-permute-start.8) | collective-permute-done | bytes 524320 | tf_op jit(solution)/shard_map/ppermute | solution.py:459
  68.0 1.5 %collective-permute-start.22 = (s32[1024,128]{1,0:T(8,128)S(1)}, s32[1024,128]{1,0:T(8,128)S(1)}, u32[]{:S(2)}, u32[]{:S(2)}) collective-permute-start(s32[1024,128]{1,0:T(8,128)S(1)} %collective-permute-done.7.refs_8_), channel_id=1, source_target_pairs={{0,16},{1,17},{2,18},{3,19},{4,20},{5,21},{6,22},{7,23},{8,9},{9,8... | collective-permute-start | bytes 1572872 | tf_op jit(solution)/shard_map/ppermute | solution.py:459
  69.5 15.7 %collective-permute-done.25.rest_9_ = s32[1024,128]{1,0:T(8,128)S(1)} collective-permute-done((s32[1024,128]{1,0:T(8,128)S(1)}, s32[1024,128]{1,0:T(8,128)S(1)}, u32[]{:S(2)}, u32[]{:S(2)}) %collective-permute-start.25) | collective-permute-done | bytes 524320 | tf_op jit(solution)/shard_map/ppermute | solution.py:459
  89.2 2.9 %lookup.5.refs_0_ = s32[128,128]{1,0:T(8,128)S(1)} custom-call(bf16[256,512]{1,0:T(8,128)(2,1)S(1)} %planes.1.planes_ref, s32[128,128]{1,0:T(8,128)S(1)} %bitcast.16), custom_call_target="tpu_custom_call" | custom-call | tf_op jit(solution)/shard_map/lookup/pallas_call | solution.py:103
  92.9 2.9 %lookup.6.refs_0_ = s32[128,128]{1,0:T(8,128)S(1)} custom-call(bf16[256,512]{1,0:T(8,128)(2,1)S(1)} %planes.1.planes_ref, s32[128,128]{1,0:T(8,128)S(1)} %bitcast.17, s32[128,128]{1,0:T(8,128)S(1)} %lookup.5.refs_0_), custom_call_target="tpu_custom_call" | custom-call | tf_op jit(solution)/shard_map/lookup/pallas_call | solution.py:103
  95.8 2.3 %lookup.7.refs_0_ = s32[128,128]{1,0:T(8,128)S(1)} custom-call(bf16[256,512]{1,0:T(8,128)(2,1)S(1)} %planes.1.planes_ref, s32[128,128]{1,0:T(8,128)S(1)} %bitcast.18, s32[128,128]{1,0:T(8,128)S(1)} %lookup.6.refs_0_), custom_call_target="tpu_custom_call" | custom-call | tf_op jit(solution)/shard_map/lookup/pallas_call | solution.py:103
  101.8 3.2 %stage.1 = (s32[32784,128]{1,0:T(8,128)S(1)}, s32[128,128]{1,0:T(8,128)S(1)}, s32[128,128]{1,0:T(8,128)S(1)}, bf16[16384,128]{1,0:T(8,128)(2,1)S(1)}) custom-call(s32[128,128]{1,0:T(8,128)S(1)} %lookup.9.home_ref, bf16[16384,128]{1,0:T(8,128)(2,1)} %child_ref.1, s32[1024,128]{1,0:T(8,128)S(1)} %pack.1.refs_0_, s32[1024,128]{1,0:T(8,128)S(1)} %collective-permute-done.refs_1_, ...), custom_call_target="tpu_custom_call" | custom-call | tf_op jit(solution)/shard_map/stage/pallas_call | solution.py:255
  105.1 15.6 %values.1 = (f32[128,128]{1,0:T(8,128)}, s32[32,8,128]{2,1,0:T(8,128)S(1)}, s32[32784,128]{1,0:T(8,128)S(1)}) custom-call(s32[16384]{0:T(1024)S(1)} %bitcast.23, s32[128,128]{1,0:T(8,128)S(1)} %get-tuple-element.15.odd_ref, bf16[16384,128]{1,0:T(8,128)(2,1)S(1)} %get-tuple-element.16.child, ...), custom_call_target="tpu_custom_call", output_to_operand_aliasing={{2}: (7, {})} | custom-call | tf_op jit(solution)/shard_map/values/pallas_call | solution.py:323
  120.8 12.7 %all_to_all.17.incoming_ref = s32[32,8,128]{2,1,0:T(8,128)S(1)} all-to-all(s32[32,8,128]{2,1,0:T(8,128)S(1)} %get-tuple-element.21), channel_id=1, replica_groups=mesh['gx'=4,'gy'=8] {'gx','gy'}, dimensions={0} | all-to-all | bytes 262144 | tf_op jit(solution)/shard_map/all_to_all | solution.py:522
  134.5 2.5 %all-to-all-start.1 = ((f32[32,1,128]{2,1,0:T(1,128)}), f32[32,1,128]{2,1,0:T(1,128)S(1)}, u32[]{:S(2)}, u32[]{:S(2)}) async-start(f32[32,1,128]{2,1,0:T(1,128)} %bitcast.10), calls=%async_computation.1 | async-start | bytes 32768 | tf_op jit(solution)/shard_map/all_to_all | solution.py:525
  137.5 6.6 %all-to-all-done.1 = f32[32,1,128]{2,1,0:T(1,128)S(1)} async-done(((f32[32,1,128]{2,1,0:T(1,128)}), f32[32,1,128]{2,1,0:T(1,128)S(1)}, u32[]{:S(2)}, u32[]{:S(2)}) %all-to-all-start.1) | async-done | bytes 16416 | tf_op jit(solution)/shard_map/all_to_all | solution.py:525
  (72 shorter events, 17.0 us)
Async XLA Ops:
  2.4 17.4 %collective-permute-start.9 = (s32[1024,128]{1,0:T(8,128)S(1)}, s32[1024,128]{1,0:T(8,128)S(1)}, u32[]{:S(2)}, u32[]{:S(2)}) collective-permute-start(s32[1024,128]{1,0:T(8,128)S(1)} %pack.1.refs_0_), channel_id=1, source_target_pairs={{0,6},{1,7},{2,0},{3,1},{4,2},{5,3},{6,4},{7,5},{8,14},{9,15},{10,... | collective-permute-start | bytes 1572872 | tf_op jit(solution)/shard_map/ppermute | solution.py:459
  7.5 13.8 %collective-permute-start.10 = (s32[1024,128]{1,0:T(8,128)S(1)}, s32[1024,128]{1,0:T(8,128)S(1)}, u32[]{:S(2)}, u32[]{:S(2)}) collective-permute-start(s32[1024,128]{1,0:T(8,128)S(1)} %pack.1.refs_0_), channel_id=1, source_target_pairs={{0,8},{1,9},{2,10},{3,11},{4,12},{5,13},{6,14},{7,15},{8,0},{9,1},... | collective-permute-start | bytes 1572872 | tf_op jit(solution)/shard_map/ppermute | solution.py:459
  7.5 23.3 %collective-permute-start.3 = (s32[1024,128]{1,0:T(8,128)S(1)}, s32[1024,128]{1,0:T(8,128)S(1)}, u32[]{:S(2)}, u32[]{:S(2)}) collective-permute-start(s32[1024,128]{1,0:T(8,128)S(1)} %pack.1.refs_0_), channel_id=1, source_target_pairs={{0,2},{1,3},{2,4},{3,5},{4,6},{5,7},{6,0},{7,1},{8,10},{9,11},{10,... | collective-permute-start | bytes 1572872 | tf_op jit(solution)/shard_map/ppermute | solution.py:459
  7.5 23.3 %collective-permute-start.1 = (s32[1024,128]{1,0:T(8,128)S(1)}, s32[1024,128]{1,0:T(8,128)S(1)}, u32[]{:S(2)}, u32[]{:S(2)}) collective-permute-start(s32[1024,128]{1,0:T(8,128)S(1)} %pack.1.refs_0_), channel_id=1, source_target_pairs={{0,16},{1,17},{2,18},{3,19},{4,20},{5,21},{6,22},{7,23},{8,9},{9,8... | collective-permute-start | bytes 1572872 | tf_op jit(solution)/shard_map/ppermute | solution.py:459
  9.1 22.3 %collective-permute-start = (s32[1024,128]{1,0:T(8,128)S(1)}, s32[1024,128]{1,0:T(8,128)S(1)}, u32[]{:S(2)}, u32[]{:S(2)}) collective-permute-start(s32[1024,128]{1,0:T(8,128)S(1)} %pack.1.refs_0_), channel_id=1, source_target_pairs={{0,1},{1,0},{2,3},{3,2},{4,5},{5,4},{6,7},{7,6},{8,24},{9,25},{10,... | collective-permute-start | bytes 1572872 | tf_op jit(solution)/shard_map/ppermute | solution.py:459
  19.8 13.7 %collective-permute-start.24 = (s32[1024,128]{1,0:T(8,128)S(1)}, s32[1024,128]{1,0:T(8,128)S(1)}, u32[]{:S(2)}, u32[]{:S(2)}) collective-permute-start(s32[1024,128]{1,0:T(8,128)S(1)} %collective-permute-done.9.refs_10_), channel_id=1, source_target_pairs={{0,16},{1,17},{2,18},{3,19},{4,20},{5,21},{6,22},{7,23},{8,9},{9,8... | collective-permute-start | bytes 1572872 | tf_op jit(solution)/shard_map/ppermute | solution.py:459
  21.4 13.7 %collective-permute-start.23 = (s32[1024,128]{1,0:T(8,128)S(1)}, s32[1024,128]{1,0:T(8,128)S(1)}, u32[]{:S(2)}, u32[]{:S(2)}) collective-permute-start(s32[1024,128]{1,0:T(8,128)S(1)} %collective-permute-done.9.refs_10_), channel_id=1, source_target_pairs={{0,1},{1,0},{2,3},{3,2},{4,5},{5,4},{6,7},{7,6},{8,24},{9,25},{10,... | collective-permute-start | bytes 1572872 | tf_op jit(solution)/shard_map/ppermute | solution.py:459
  31.4 15.7 %collective-permute-start.6 = (s32[1024,128]{1,0:T(8,128)S(1)}, s32[1024,128]{1,0:T(8,128)S(1)}, u32[]{:S(2)}, u32[]{:S(2)}) collective-permute-start(s32[1024,128]{1,0:T(8,128)S(1)} %collective-permute-done.3.refs_4_), channel_id=1, source_target_pairs={{0,2},{1,3},{2,4},{3,5},{4,6},{5,7},{6,0},{7,1},{8,10},{9,11},{10,... | collective-permute-start | bytes 1572872 | tf_op jit(solution)/shard_map/ppermute | solution.py:459
  33.6 15.0 %collective-permute-start.5 = (s32[1024,128]{1,0:T(8,128)S(1)}, s32[1024,128]{1,0:T(8,128)S(1)}, u32[]{:S(2)}, u32[]{:S(2)}) collective-permute-start(s32[1024,128]{1,0:T(8,128)S(1)} %collective-permute-done.3.refs_4_), channel_id=1, source_target_pairs={{0,16},{1,17},{2,18},{3,19},{4,20},{5,21},{6,22},{7,23},{8,9},{9,8... | collective-permute-start | bytes 1572872 | tf_op jit(solution)/shard_map/ppermute | solution.py:459
  35.1 13.5 %collective-permute-start.4 = (s32[1024,128]{1,0:T(8,128)S(1)}, s32[1024,128]{1,0:T(8,128)S(1)}, u32[]{:S(2)}, u32[]{:S(2)}) collective-permute-start(s32[1024,128]{1,0:T(8,128)S(1)} %collective-permute-done.3.refs_4_), channel_id=1, source_target_pairs={{0,1},{1,0},{2,3},{3,2},{4,5},{5,4},{6,7},{7,6},{8,24},{9,25},{10,... | collective-permute-start | bytes 1572872 | tf_op jit(solution)/shard_map/ppermute | solution.py:459
  36.4 14.3 %collective-permute-start.11 = (s32[1024,128]{1,0:T(8,128)S(1)}, s32[1024,128]{1,0:T(8,128)S(1)}, u32[]{:S(2)}, u32[]{:S(2)}) collective-permute-start(s32[1024,128]{1,0:T(8,128)S(1)} %collective-permute-done.refs_1_), channel_id=1, source_target_pairs={{0,8},{1,9},{2,10},{3,11},{4,12},{5,13},{6,14},{7,15},{8,0},{9,1},... | collective-permute-start | bytes 1572872 | tf_op jit(solution)/shard_map/ppermute | solution.py:459
  48.6 18.9 %collective-permute-start.8 = (s32[1024,128]{1,0:T(8,128)S(1)}, s32[1024,128]{1,0:T(8,128)S(1)}, u32[]{:S(2)}, u32[]{:S(2)}) collective-permute-start(s32[1024,128]{1,0:T(8,128)S(1)} %collective-permute-done.6.refs_7_), channel_id=1, source_target_pairs={{0,16},{1,17},{2,18},{3,19},{4,20},{5,21},{6,22},{7,23},{8,9},{9,8... | collective-permute-start | bytes 1572872 | tf_op jit(solution)/shard_map/ppermute | solution.py:459
  49.3 18.1 %collective-permute-start.7 = (s32[1024,128]{1,0:T(8,128)S(1)}, s32[1024,128]{1,0:T(8,128)S(1)}, u32[]{:S(2)}, u32[]{:S(2)}) collective-permute-start(s32[1024,128]{1,0:T(8,128)S(1)} %collective-permute-done.6.refs_7_), channel_id=1, source_target_pairs={{0,1},{1,0},{2,3},{3,2},{4,5},{5,4},{6,7},{7,6},{8,24},{9,25},{10,... | collective-permute-start | bytes 1572872 | tf_op jit(solution)/shard_map/ppermute | solution.py:459
  50.7 16.8 %collective-permute-start.16 = (s32[1024,128]{1,0:T(8,128)S(1)}, s32[1024,128]{1,0:T(8,128)S(1)}, u32[]{:S(2)}, u32[]{:S(2)}) collective-permute-start(s32[1024,128]{1,0:T(8,128)S(1)} %collective-permute-done.5.refs_6_), channel_id=1, source_target_pairs={{0,8},{1,9},{2,10},{3,11},{4,12},{5,13},{6,14},{7,15},{8,0},{9,1},... | collective-permute-start | bytes 1572872 | tf_op jit(solution)/shard_map/ppermute | solution.py:459
  59.6 25.6 %collective-permute-start.25 = (s32[1024,128]{1,0:T(8,128)S(1)}, s32[1024,128]{1,0:T(8,128)S(1)}, u32[]{:S(2)}, u32[]{:S(2)}) collective-permute-start(s32[1024,128]{1,0:T(8,128)S(1)} %collective-permute-done.2.refs_3_), channel_id=1, source_target_pairs={{0,6},{1,7},{2,0},{3,1},{4,2},{5,3},{6,4},{7,5},{8,14},{9,15},{10,... | collective-permute-start | bytes 1572872 | tf_op jit(solution)/shard_map/ppermute | solution.py:459
  67.5 17.7 %collective-permute-start.21 = (s32[1024,128]{1,0:T(8,128)S(1)}, s32[1024,128]{1,0:T(8,128)S(1)}, u32[]{:S(2)}, u32[]{:S(2)}) collective-permute-start(s32[1024,128]{1,0:T(8,128)S(1)} %collective-permute-done.2.refs_3_), channel_id=1, source_target_pairs={{0,2},{1,3},{2,4},{3,5},{4,6},{5,7},{6,0},{7,1},{8,10},{9,11},{10,... | collective-permute-start | bytes 1572872 | tf_op jit(solution)/shard_map/ppermute | solution.py:459
  67.5 18.2 %collective-permute-start.13 = (s32[1024,128]{1,0:T(8,128)S(1)}, s32[1024,128]{1,0:T(8,128)S(1)}, u32[]{:S(2)}, u32[]{:S(2)}) collective-permute-start(s32[1024,128]{1,0:T(8,128)S(1)} %collective-permute-done.2.refs_3_), channel_id=1, source_target_pairs={{0,8},{1,9},{2,10},{3,11},{4,12},{5,13},{6,14},{7,15},{8,0},{9,1},... | collective-permute-start | bytes 1572872 | tf_op jit(solution)/shard_map/ppermute | solution.py:459
  67.5 18.3 %collective-permute-start.19 = (s32[1024,128]{1,0:T(8,128)S(1)}, s32[1024,128]{1,0:T(8,128)S(1)}, u32[]{:S(2)}, u32[]{:S(2)}) collective-permute-start(s32[1024,128]{1,0:T(8,128)S(1)} %collective-permute-done.8.refs_9_), channel_id=1, source_target_pairs={{0,8},{1,9},{2,10},{3,11},{4,12},{5,13},{6,14},{7,15},{8,0},{9,1},... | collective-permute-start | bytes 1572872 | tf_op jit(solution)/shard_map/ppermute | solution.py:459
  68.0 18.2 %collective-permute-start.22 = (s32[1024,128]{1,0:T(8,128)S(1)}, s32[1024,128]{1,0:T(8,128)S(1)}, u32[]{:S(2)}, u32[]{:S(2)}) collective-permute-start(s32[1024,128]{1,0:T(8,128)S(1)} %collective-permute-done.7.refs_8_), channel_id=1, source_target_pairs={{0,16},{1,17},{2,18},{3,19},{4,20},{5,21},{6,22},{7,23},{8,9},{9,8... | collective-permute-start | bytes 1572872 | tf_op jit(solution)/shard_map/ppermute | solution.py:459
  85.2 19.9 %collective-permute-start.29 = (s32[1024,128]{1,0:T(8,128)S(1)}, s32[1024,128]{1,0:T(8,128)S(1)}, u32[]{:S(2)}, u32[]{:S(2)}) collective-permute-start(s32[1024,128]{1,0:T(8,128)S(1)} %collective-permute-done.24.rest_8_), channel_id=1, source_target_pairs={{0,8},{1,9},{2,10},{3,11},{4,12},{5,13},{6,14},{7,15},{8,0},{9,1},... | collective-permute-start | bytes 1572872 | tf_op jit(solution)/shard_map/ppermute | solution.py:459
  85.7 19.4 %collective-permute-start.28 = (s32[1024,128]{1,0:T(8,128)S(1)}, s32[1024,128]{1,0:T(8,128)S(1)}, u32[]{:S(2)}, u32[]{:S(2)}) collective-permute-start(s32[1024,128]{1,0:T(8,128)S(1)} %collective-permute-done.23.rest_7_), channel_id=1, source_target_pairs={{0,8},{1,9},{2,10},{3,11},{4,12},{5,13},{6,14},{7,15},{8,0},{9,1},... | collective-permute-start | bytes 1572872 | tf_op jit(solution)/shard_map/ppermute | solution.py:459
  85.8 19.3 %collective-permute-start.30 = (s32[1024,128]{1,0:T(8,128)S(1)}, s32[1024,128]{1,0:T(8,128)S(1)}, u32[]{:S(2)}, u32[]{:S(2)}) collective-permute-start(s32[1024,128]{1,0:T(8,128)S(1)} %collective-permute-done.25.rest_9_), channel_id=1, source_target_pairs={{0,8},{1,9},{2,10},{3,11},{4,12},{5,13},{6,14},{7,15},{8,0},{9,1},... | collective-permute-start | bytes 1572872 | tf_op jit(solution)/shard_map/ppermute | solution.py:459
  86.2 18.9 %collective-permute-start.26 = (s32[1024,128]{1,0:T(8,128)S(1)}, s32[1024,128]{1,0:T(8,128)S(1)}, u32[]{:S(2)}, u32[]{:S(2)}) collective-permute-start(s32[1024,128]{1,0:T(8,128)S(1)} %collective-permute-done.21.rest_5_), channel_id=1, source_target_pairs={{0,8},{1,9},{2,10},{3,11},{4,12},{5,13},{6,14},{7,15},{8,0},{9,1},... | collective-permute-start | bytes 1572872 | tf_op jit(solution)/shard_map/ppermute | solution.py:459
  87.1 18.0 %collective-permute-start.27 = (s32[1024,128]{1,0:T(8,128)S(1)}, s32[1024,128]{1,0:T(8,128)S(1)}, u32[]{:S(2)}, u32[]{:S(2)}) collective-permute-start(s32[1024,128]{1,0:T(8,128)S(1)} %collective-permute-done.22.rest_6_), channel_id=1, source_target_pairs={{0,8},{1,9},{2,10},{3,11},{4,12},{5,13},{6,14},{7,15},{8,0},{9,1},... | collective-permute-start | bytes 1572872 | tf_op jit(solution)/shard_map/ppermute | solution.py:459
  (17 other events, 309.6 us)
